TPU v7x, 512 devices: a whole 4x8x8 slice. The times are simulated.
512 devices in a mesh: dp: 8 (over y), expert: 64 (over z, x, core).
Axes of the slice: x: 4, y: 8, z: 8, core: 2. Of those that a mesh axis runs over, the one named last changes fastest.
Arguments:
- tokens: bfloat16 [4096, 2880], P(('dp', 'expert')), may hold values from -6 to 6
- routes: int32 [2, 4096, 4], P(None, ('dp', 'expert')), may hold values from 0 to 63, all different within a row; in each aligned block of 8 rows (0 to 7, 8 to 15, ..., all dimensions but the last counted through in order) at most 1 rows name the same one
- placement: int32 [2, 64], replicated, may hold values from 0 to 63, each once within a row
- up_weight: bfloat16 [2, 64, 2880, 1440], P(None, 'expert', None, 'dp'), may hold values from -0.109375 to 0.109375
- down_weight: bfloat16 [2, 64, 1440, 2880], P(None, 'expert', 'dp'), may hold values from -0.15625 to 0.15625
- router_weight: bfloat16 [2, 64, 2880], P(None, 'expert'), may hold values from -0.21875 to 0.21875
Outputs:
- final_stream: bfloat16 [4096, 2880], P(('dp', 'expert'))
Inputs may be any that keep to these rules, and one draw needn't show every extreme that they name: `routes`: each row names 4 different experts. Within one layer's rows of one device no expert is named by more than 1 row, and some device names some expert exactly 1 times. `placement`: each layer's row is a permutation of the slots.
All inputs are finite; a program needn't handle non-finite values.
Results may differ from a plain program's by a relative error of at most 0.008.
Values may be sent and summed in bfloat16 or wider, within the bound.
A program may use at most 64 MiB of HBM per device.

v0:
```python
from functools import partial

import jax
import jax.numpy as jnp
from jax import lax
from jax.sharding import PartitionSpec as P


def from_everyone(value, axis):
    count = lax.axis_size(axis)
    return lax.all_to_all(
        jnp.broadcast_to(value[None], (count, *value.shape)), axis, 0, 0, tiled=True
    )


def joined_along(parts, dim):
    parts = jnp.moveaxis(parts, 0, dim)
    lengths = parts.shape
    return parts.reshape(*lengths[:dim], lengths[dim] * lengths[dim + 1], *lengths[dim + 2 :])


def gather_directly(value, axis, dim):
    parts = from_everyone(value, axis)
    return joined_along(parts, dim)


def side_by_side(arrays, axis, split_dim, concat_dim, along):
    columns = [a.reshape(*a.shape[:along], -1) for a in arrays]
    both = jnp.concatenate(columns, axis=along)
    whole, at, done = (
        lax.all_to_all(both, axis, split_axis=split_dim, concat_axis=concat_dim, tiled=True),
        0,
        [],
    )
    for a, column in zip(arrays, columns):
        slab = whole[..., at : at + column.shape[along]]
        done.append(slab.reshape(*slab.shape[:along], *a.shape[along:]))
        at += column.shape[along]
    return tuple(done)


def cut_along(value, dim, count):
    before, after = (value.shape[:dim], value.shape[dim + 1 :])
    return jnp.moveaxis(value.reshape(*before, count, -1, *after), dim, 0)


def sent_and_summed(value, axis, dim):
    count = lax.axis_size(axis)
    parts = lax.all_to_all(cut_along(value, dim, count), axis, 0, 0, tiled=True)
    return jnp.sum(parts.astype(jnp.float32), axis=0)


def rms_rows(stream):
    values = stream.astype(jnp.float32)
    inverse = lax.rsqrt(jnp.mean(values * values, axis=-1, keepdims=True) + 1e-05)
    return (values * inverse).astype(jnp.bfloat16)


def slot_table(route_rows, place_row, columns, capacity):
    tok_rows, top_k = route_rows.shape
    experts = place_row.shape[0]
    matches = route_rows[:, :, None] == jnp.arange(experts, dtype=jnp.int32)[None, None, :]
    target = jnp.sum(jnp.where(matches, place_row[None, None, :], 0), axis=2).reshape(-1)
    row_count = target.shape[0]
    positions = jnp.arange(row_count, dtype=jnp.int32)
    earlier = (positions[None, :] < positions[:, None]) & (target[None, :] == target[:, None])
    row_rank = jnp.sum(earlier.astype(jnp.int32), axis=1)
    placed = (target[:, None, None] == jnp.arange(columns, dtype=jnp.int32)[None, :, None]) & (
        row_rank[:, None, None] == jnp.arange(capacity, dtype=jnp.int32)[None, None, :]
    )
    slot_map = jnp.sum(
        placed.reshape(tok_rows, top_k, columns, capacity).astype(jnp.float32), axis=1
    )
    return jnp.transpose(slot_map, (1, 2, 0))


def per_device(tokens, routes, placement, up_weight, down_weight, router_weight):
    groups = lax.axis_size("dp")
    columns = lax.axis_size("expert")
    tok_rows = tokens.shape[0]
    top_k = routes.shape[2]
    capacity = 2 * tok_rows * top_k // columns
    own_group = 0
    route_source = gather_directly(routes, "dp", 1)
    own_group = lax.axis_index("dp")

    def layer_step(stream, packed):
        route_rows, place_row, up_part, down_part, router_part = packed
        normed = rms_rows(stream)
        grouped = route_rows.reshape(groups, tok_rows, top_k)
        group_maps = jax.vmap(
            partial(slot_table, columns=columns, capacity=capacity), in_axes=(0, None)
        )(grouped, place_row)
        slot_map = lax.dynamic_index_in_dim(group_maps, own_group, 0, keepdims=False)
        outgoing = jnp.einsum(
            "jct,td->jcd", slot_map.astype(jnp.bfloat16), normed, preferred_element_type=jnp.float32
        ).astype(jnp.bfloat16)
        arrived = lax.all_to_all(
            outgoing, "expert", split_axis=0, concat_axis=0, tiled=True
        ).reshape(columns * capacity, -1)
        affinity = jax.nn.sigmoid(
            jnp.dot(arrived, router_part[0], preferred_element_type=jnp.float32)
        ).astype(jnp.bfloat16)
        all_rows, all_gates = (
            lax.all_gather(arrived, "dp", axis=0, tiled=True),
            lax.all_gather(affinity, "dp", axis=0, tiled=True),
        )
        hidden = jax.nn.silu(
            jnp.dot(all_rows, up_part[0], preferred_element_type=jnp.float32)
        ).astype(jnp.bfloat16)
        part_sums = jnp.dot(hidden, down_part[0], preferred_element_type=jnp.float32).astype(
            jnp.bfloat16
        )
        part_sums = part_sums.reshape(groups, columns, capacity, -1)
        all_gates = all_gates.reshape(groups, columns, capacity)
        returned, gates_back = side_by_side((part_sums, all_gates), "expert", 1, 1, 3)
        weights = group_maps * gates_back.astype(jnp.float32)[:, :, :, None]
        owner_terms = jnp.einsum(
            "gect,gecd->gtd",
            weights.astype(jnp.bfloat16),
            returned,
            preferred_element_type=jnp.float32,
        )
        numerator = sent_and_summed(owner_terms.astype(jnp.bfloat16), "dp", 0)[0]
        own_weights = lax.dynamic_index_in_dim(weights, own_group, 0, keepdims=False)
        denominator = jnp.sum(own_weights, axis=(0, 1))
        updated = stream.astype(jnp.float32) + numerator / jnp.maximum(denominator, 0.5)[:, None]
        return (updated.astype(jnp.bfloat16), None)

    result_stream, unused = lax.scan(
        layer_step, tokens, (route_source, placement, up_weight, down_weight, router_weight)
    )
    return result_stream


def solution(mesh):
    return jax.shard_map(
        per_device,
        mesh=mesh,
        in_specs=(
            P(("dp", "expert"), None),
            P(None, ("dp", "expert"), None),
            P(),
            P(None, "expert", None, "dp"),
            P(None, "expert", "dp", None),
            P(None, "expert", None),
        ),
        out_specs=P(("dp", "expert"), None),
        check_vma=False,
    )
```

profile of v0, /device:TPU:1, one launch (start us, length us, event | category | flops | bytes accessed | tf_op | source)
XLA Modules:
  0.0 395.3 jit_solution(9854523064462696396)
XLA Ops:
  6.5 1.5 broadcast_in_dim.20
  8.0 7.6 %all-to-all-start.3 = ((s32[8,2,8,4]{2,3,1,0:T(4,128)}), s32[8,2,8,4]{2,3,1,0:T(4,128)S(1)}, u32[]{:S(2)}, u32[]{:S(2)}) async-start(s32[8,2,8,4]{2,3,1,0:T(4,128)} %broadcast_in_dim.20), calls=%async_computation.3 | async-start | bytes 65536 | tf_op jit(solution)/shard_map/all_to_all | solution.py:11
  15.6 3.1 copy.80
  18.8 1.6 copy.81
  20.4 2.1 all-to-all-done.3
  22.7 365.1 %while.12 = (s32[]{:T(128)}, bf16[8,2880]{1,0:T(8,128)(2,1)S(1)}, s32[2,64,4]{1,2,0:T(4,128)S(1)}, s32[2,64]{1,0:T(2,128)S(1)}, s32[]{:T(128)}, /*index=5*/bf16[...) while((s32[]{:T(128)}, bf16[8,2880]{1,0:T(8,128)(2,1)S(1)}, ...), condition=%wide.region_7.8_spmd, body=%wide.region_0.7_spmd.sunk | while | flops 1097528320 | bytes 51477372 | solution.py:130
  25.4 0.8 reduce.13
  26.7 30.3 %all_to_all.29 = bf16[64,2,1440]{2,1,0:T(2,128)(2,1)S(1)} all-to-all(bf16[64,2,1440]{2,1,0:T(2,128)(2,1)S(1)} %reshape.159), channel_id=1, replica_groups=mesh['dp'=8,'expert'=64] {'expert'}, dimensions={0} | all-to-all | bytes 737280 | tf_op jit(solution)/shard_map/while/body/eval_jaxpr/all_to_all | solution.py:98
  58.4 1.3 dynamic-slice.20
  60.4 1.2 fusion.66
  61.8 11.9 %all-reduce.2 = bf16[512]{0:T(512)(128)(2,1)S(1)} all-reduce(bf16[512]{0:T(512)(128)(2,1)S(1)} %dynamic-update-slice.2), channel_id=1, replica_groups=mesh['dp'=8,'expert'=64] {'dp'}, use_global_device_ids=true, to_apply=%add | all-reduce | flops 512 | bytes 2048 | tf_op jit(solution)/shard_map/while
  74.0 22.8 %all-gather.5.cloned.1.call-done = bf16[512,1,2880]{2,0,1:T(8,128)(2,1)} async-done(((bf16[64,1,2880]{2,0,1:T(8,128)(2,1)}), bf16[512,1,2880]{2,0,1:T(8,128)(2,1)}) %all-gather.5.cloned.1.call-update) | async-done | bytes 2949136 | tf_op jit(solution)/shard_map/while/body/eval_jaxpr/all_gather | solution.py:105
  96.8 6.2 %convolution_convert_fusion.4 = bf16[512,2880]{0,1:T(8,128)(2,1)} fusion(bf16[2,1,180,2880]{3,2,1,0:T(8,128)(2,1)} %get-tuple-element.241, s32[]{:T(128)} %get-tuple-element.221, bf16[2,1,2880,180]{2,3,1,0:T(8,128)(2,1)} %get-tuple-element.240, bf16[512,1,2880]{2,0,1:T(8,128)(2,1)} %all-gather.5.cloned.1.call-done), kind=kOutput, calls=%fused_computation.clone.1 | convolution fusion | flops 1063618560 | bytes 8131584 | tf_op jit(solution)/shard_map/while/body/eval_jaxpr/dot_general | solution.py:111
  103.1 3.3 copy.108
  106.9 1.7 copy.109
  108.5 82.8 %all_to_all.30 = bf16[8,64,1,2881]{3,0,2,1:T(8,128)(2,1)S(1)} all-to-all(bf16[8,64,1,2881]{3,0,2,1:T(8,128)(2,1)S(1)} %copy.109), channel_id=1, replica_groups=mesh['dp'=8,'expert'=64] {'expert'}, dimensions={1} | all-to-all | bytes 5900288 | tf_op jit(solution)/shard_map/while/body/eval_jaxpr/all_to_all | solution.py:31
  191.6 1.6 fusion.67
  193.2 3.8 all-to-all-start.2
  197.2 13.0 %all-to-all-done.2 = bf16[8,1,8,2880]{3,2,1,0:T(8,128)(2,1)S(1)} async-done(((bf16[8,1,8,2880]{3,2,1,0:T(8,128)(2,1)}), bf16[8,1,8,2880]{3,2,1,0:T(8,128)(2,1)S(1)}, u32[]{:S(2)}, u32[]{:S(2)}) %all-to-all-start.2) | async-done | bytes 368672 | tf_op jit(solution)/shard_map/while/body/eval_jaxpr/all_to_all | solution.py:49
  213.0 0.8 reduce.13
  214.3 22.4 %all_to_all.29 = bf16[64,2,1440]{2,1,0:T(2,128)(2,1)S(1)} all-to-all(bf16[64,2,1440]{2,1,0:T(2,128)(2,1)S(1)} %reshape.159), channel_id=1, replica_groups=mesh['dp'=8,'expert'=64] {'expert'}, dimensions={0} | all-to-all | bytes 737280 | tf_op jit(solution)/shard_map/while/body/eval_jaxpr/all_to_all | solution.py:98
  238.1 1.3 dynamic-slice.20
  240.0 1.2 fusion.66
  241.5 12.1 %all-reduce.2 = bf16[512]{0:T(512)(128)(2,1)S(1)} all-reduce(bf16[512]{0:T(512)(128)(2,1)S(1)} %dynamic-update-slice.2), channel_id=1, replica_groups=mesh['dp'=8,'expert'=64] {'dp'}, use_global_device_ids=true, to_apply=%add | all-reduce | flops 512 | bytes 2048 | tf_op jit(solution)/shard_map/while
  253.9 20.7 %all-gather.5.cloned.1.call-done = bf16[512,1,2880]{2,0,1:T(8,128)(2,1)} async-done(((bf16[64,1,2880]{2,0,1:T(8,128)(2,1)}), bf16[512,1,2880]{2,0,1:T(8,128)(2,1)}) %all-gather.5.cloned.1.call-update) | async-done | bytes 2949136 | tf_op jit(solution)/shard_map/while/body/eval_jaxpr/all_gather | solution.py:105
  274.5 6.2 %convolution_convert_fusion.4 = bf16[512,2880]{0,1:T(8,128)(2,1)} fusion(bf16[2,1,180,2880]{3,2,1,0:T(8,128)(2,1)} %get-tuple-element.241, s32[]{:T(128)} %get-tuple-element.221, bf16[2,1,2880,180]{2,3,1,0:T(8,128)(2,1)} %get-tuple-element.240, bf16[512,1,2880]{2,0,1:T(8,128)(2,1)} %all-gather.5.cloned.1.call-done), kind=kOutput, calls=%fused_computation.clone.1 | convolution fusion | flops 1063618560 | bytes 8131584 | tf_op jit(solution)/shard_map/while/body/eval_jaxpr/dot_general | solution.py:111
  280.8 3.3 copy.108
  284.6 1.7 copy.109
  286.2 82.6 %all_to_all.30 = bf16[8,64,1,2881]{3,0,2,1:T(8,128)(2,1)S(1)} all-to-all(bf16[8,64,1,2881]{3,0,2,1:T(8,128)(2,1)S(1)} %copy.109), channel_id=1, replica_groups=mesh['dp'=8,'expert'=64] {'expert'}, dimensions={1} | all-to-all | bytes 5900288 | tf_op jit(solution)/shard_map/while/body/eval_jaxpr/all_to_all | solution.py:31
  369.1 1.6 fusion.67
  370.7 3.8 all-to-all-start.2
  374.7 13.0 %all-to-all-done.2 = bf16[8,1,8,2880]{3,2,1,0:T(8,128)(2,1)S(1)} async-done(((bf16[8,1,8,2880]{3,2,1,0:T(8,128)(2,1)}), bf16[8,1,8,2880]{3,2,1,0:T(8,128)(2,1)S(1)}, u32[]{:S(2)}, u32[]{:S(2)}) %all-to-all-start.2) | async-done | bytes 368672 | tf_op jit(solution)/shard_map/while/body/eval_jaxpr/all_to_all | solution.py:49
  (80 shorter events, 12.7 us)
Async XLA Ops:
  6.5 12.2 %copy-start.2 = (bf16[2,1,180,2880]{3,0,2,1:T(2,128)(2,1)S(1)}, bf16[2,1,180,2880]{3,0,2,1:T(2,128)(2,1)}, u32[]{:S(2)}) copy-start(bf16[2,1,180,2880]{3,0,2,1:T(2,128)(2,1)} %param.12) | copy-start | bytes 6220804
  8.0 14.6 %all-to-all-start.3 = ((s32[8,2,8,4]{2,3,1,0:T(4,128)}), s32[8,2,8,4]{2,3,1,0:T(4,128)S(1)}, u32[]{:S(2)}, u32[]{:S(2)}) async-start(s32[8,2,8,4]{2,3,1,0:T(4,128)} %broadcast_in_dim.20), calls=%async_computation.3 | async-start | bytes 65536 | tf_op jit(solution)/shard_map/all_to_all | solution.py:11
  18.8 3.9 copy-start.1
  18.8 3.9 copy-start.3
  18.8 3.9 copy-start.4
  22.7 74.1 %all-gather.5.cloned.1.call-start = ((), (), s32[]{:S(2)}) async-start(), calls=%async_computation.4 | async-start | bytes 3391488 | tf_op jit(solution)/shard_map/while/body/eval_jaxpr/all_gather | solution.py:105
  193.2 16.9 %all-to-all-start.2 = ((bf16[8,1,8,2880]{3,2,1,0:T(8,128)(2,1)}), bf16[8,1,8,2880]{3,2,1,0:T(8,128)(2,1)S(1)}, u32[]{:S(2)}, u32[]{:S(2)}) async-start(bf16[8,1,8,2880]{3,2,1,0:T(8,128)(2,1)} %fusion.67), calls=%async_computation.2 | async-start | bytes 753664 | tf_op jit(solution)/shard_map/while/body/eval_jaxpr/all_to_all | solution.py:49
  210.3 64.2 %all-gather.5.cloned.1.call-start = ((), (), s32[]{:S(2)}) async-start(), calls=%async_computation.4 | async-start | bytes 3391488 | tf_op jit(solution)/shard_map/while/body/eval_jaxpr/all_gather | solution.py:105
  370.7 16.9 %all-to-all-start.2 = ((bf16[8,1,8,2880]{3,2,1,0:T(8,128)(2,1)}), bf16[8,1,8,2880]{3,2,1,0:T(8,128)(2,1)S(1)}, u32[]{:S(2)}, u32[]{:S(2)}) async-start(bf16[8,1,8,2880]{3,2,1,0:T(8,128)(2,1)} %fusion.67), calls=%async_computation.2 | async-start | bytes 753664 | tf_op jit(solution)/shard_map/while/body/eval_jaxpr/all_to_all | solution.py:49
  387.8 0.6 copy-start
Sparse Core Ops, SparseCore 0:
  58.6 38.2 all-gather.4
  238.2 36.2 all-gather.4
where the time goes:
time: 396 us; the launch traced here: 395 us
  blocking collectives  242 us (61%)
  waiting for transfers between devices  71.6 us (18%)
  local copies, waits for them, and re-layouts  26.6 us (7%)
  matrix products  18.8 us (5%)
  starting transfers between devices  15.4 us (4%)
  between operations  13.4 us (3%)
  other arithmetic  5.7 us (1%)
    all_to_all x2, blocking collectives, side_by_side(): lax.all_to_all(both, axis, split_axis=split_dim, concat_axis=concat_dim,...  165 us
    all_to_all x2, blocking collectives, layer_step(): lax.all_to_all(outgoing, 'expert', split_axis=0, concat_axis=0, tiled=True)  52.7 us
    all_gather x2, waiting for transfers between devices, layer_step(): lax.all_gather(arrived, 'dp', axis=0, tiled=True)  43.5 us
    all_to_all x2, waiting for transfers between devices, sent_and_summed(): parts = lax.all_to_all(cut_along(value, dim, count), axis, 0, 0, tiled=True)  26 us
    while x2, blocking collectives  24.1 us
    dot_general x2, matrix products, layer_step(): jnp.dot(hidden, down_part[0], preferred_element_type=jnp.float32)  12.5 us
  transfers between devices with their start and end apart: 5, of which 5 were waited for; matrix products, arithmetic and copies ran while one was open for 3% of the time, Pallas kernels for 0%

commit v1 on v0

v1 whole, which is shorter than its diff:
```python
import functools

import jax
import jax.numpy as jnp
from jax import lax
from jax.experimental import pallas as pl
from jax.experimental.pallas import tpu as pltpu
from jax.sharding import PartitionSpec as P

MESH = pl.DeviceIdType.MESH
F32, BF16 = jnp.float32, jnp.bfloat16
NT = (((1,), (1,)), ((), ()))


def flat(value):
    width = value.shape[-1]
    return value.astype(F32).reshape(-1, width).astype(BF16)


def flat32(value):
    return value.astype(F32).reshape(-1, value.shape[-1])


def hops(direction, half, n):
    return n // 2 if (direction == 1) == (half == 0) else n // 2 - 1


def kernel(
    dims,
    tokens,
    routes,
    placement,
    router,
    up,
    down,
    out,
    stream,
    hot,
    up_v,
    down_v,
    router_v,
    zin1,
    xo1,
    rows1,
    toks2,
    xo2,
    rows2,
    h1,
    h2,
    hid1,
    hid2,
    gate1,
    gate2,
    part1,
    comb2,
    rs1o,
    rs1i,
    xr1o,
    xr1i,
    zr1o,
    zr1i,
    xr2o,
    xr2i,
    rs2o,
    rs2i,
    yr2o,
    yr2i,
    weight_sem,
    send_sem,
    z1_sem,
    x1_sem,
    ring1_sem,
    y2_sem,
    ring2_sem,
    x2_sem,
    rs1_sem,
    xr1_sem,
    zr1_sem,
    xr2_sem,
    rs2_sem,
    yr2_sem,
):
    ny, nz, nj, layers, features, w1, f2, ff = dims
    hj, hy = nj // 2, ny // 2
    y = lax.axis_index("dp")
    e = lax.axis_index("expert")
    z, j = e // nj, e % nj
    lanes = 128

    def at_y(other):
        return (other, e)

    def at_z(other):
        return (y, other * nj + j)

    def at_j(other):
        return (y, z * nj + other)

    def turn(a, n):
        return lax.rem(a + 2 * n, n)

    barrier = pltpu.get_barrier_semaphore()
    for d in range(1, ny):
        pl.semaphore_signal(barrier, inc=1, device_id=at_y(turn(y + d, ny)), device_id_type=MESH)
    for d in range(1, nz):
        pl.semaphore_signal(barrier, inc=1, device_id=at_z(turn(z + d, nz)), device_id_type=MESH)
    for d in range(1, nj):
        pl.semaphore_signal(barrier, inc=1, device_id=at_j(turn(j + d, nj)), device_id_type=MESH)

    weights = []
    for layer in range(layers):
        weights.append(
            (
                pltpu.make_async_copy(up.at[layer, 0], up_v.at[layer], weight_sem.at[layer, 0]),
                pltpu.make_async_copy(down.at[layer, 0], down_v.at[layer], weight_sem.at[layer, 1]),
            )
        )
        for copy in weights[-1]:
            copy.start()

    for layer in range(layers):
        picks = routes[layer]
        count = placement.shape[1]
        names = lax.broadcasted_iota(jnp.int32, (picks.shape[0], count), 1)
        named = jnp.zeros((picks.shape[0], count), F32)
        for k in range(picks.shape[1]):
            named = named + jnp.where(picks[:, k : k + 1] == names, 1.0, 0.0)
        slot_of = jnp.broadcast_to(placement[layer : layer + 1, :], (lanes, count))
        slots = lax.broadcasted_iota(jnp.int32, (lanes, count), 0)
        for which, shift in ((0, 0), (1, lanes // 2)):
            serves = jnp.where(slot_of + shift == slots, 1.0, 0.0).astype(BF16)
            hot[layer, which] = lax.dot_general(
                named.astype(BF16), serves, NT, preferred_element_type=F32
            )
    for layer in range(layers):
        gate_row = jnp.broadcast_to(router[layer].astype(F32), (lanes, features)).astype(BF16)
        router_v[layer, :, 0:features] = gate_row

    stream[...] = jnp.zeros_like(stream)
    stream[:, 0:features] = tokens[...].astype(F32)

    def picker(blocks, low):
        rows = nj * blocks
        tokens_in = blocks * 8
        return rows, tokens_in, low

    def pick_matrix(hots, blocks, low):
        rows, columns, low = picker(blocks, low)
        row = lax.broadcasted_iota(jnp.int32, (rows, lanes), 0)
        slot = lax.broadcasted_iota(jnp.int32, (rows, lanes), 1)
        wanted = jnp.where(slot == low + z * nj + row // blocks, 1.0, 0.0).astype(BF16)
        same = (
            lax.broadcasted_iota(jnp.int32, (rows, columns), 0) % blocks
            == lax.broadcasted_iota(jnp.int32, (rows, columns), 1) // 8
        )
        product = lax.dot_general(wanted, hots, NT, preferred_element_type=F32)
        return jnp.where(same, product, 0.0).astype(BF16)

    def place_matrix(hots, blocks, low):
        rows, columns, low = picker(blocks, low)
        row = lax.broadcasted_iota(jnp.int32, (rows, lanes), 0)
        slot = lax.broadcasted_iota(jnp.int32, (rows, lanes), 1)
        wanted = jnp.where(slot == low + z * nj + row // blocks, 1.0, 0.0).astype(BF16)
        same = (
            lax.broadcasted_iota(jnp.int32, (columns, rows), 1) % blocks
            == lax.broadcasted_iota(jnp.int32, (columns, rows), 0) // 8
        )
        product = lax.dot_general(hots, wanted, NT, preferred_element_type=F32)
        return jnp.where(same, product, 0.0).astype(BF16)

    def send(src, dst, sent, landed, device):
        pltpu.make_async_remote_copy(
            src_ref=src, dst_ref=dst, send_sem=sent, recv_sem=landed, device_id=device, device_id_type=MESH
        ).start()

    def wait_bytes(ref, sem):
        pltpu.make_async_copy(ref, ref, sem).wait()

    (S_Z1, S_X1, S_RING1, S_Y2, S_RING2, S_X2, S_RS1, S_XR1, S_ZR1, S_XR2, S_RS2, S_YR2) = range(12)

    def layer_body(l, carry):
        sent = lambda which: send_sem.at[l, which]

        values = stream[...]
        mean = jnp.sum(values * values, axis=1, keepdims=True) * (1.0 / features)
        normed = values * lax.rsqrt(mean + 1e-05)
        zin1[l, z, :, 0:w1] = normed[:, 0:w1].astype(BF16)
        zin1[l, z, :, w1 : w1 + lanes] = hot[l, 0].astype(BF16)
        width2 = normed.shape[1] - w1
        toks2[l, z, y, :, 0 : width2 - lanes] = normed[:, w1 : w1 + width2 - lanes].astype(BF16)
        toks2[l, z, y, :, width2 - lanes : width2] = (normed[:, w1 + width2 - lanes :] + hot[l, 1]).astype(BF16)

        @pl.when(l == 0)
        def _():
            pl.semaphore_wait(barrier, ny + nz + nj - 3)

        for d in range(1, ny):
            block = toks2.at[l, z, y]
            send(block, block, sent(S_Y2), y2_sem.at[l], at_y(turn(y + d, ny)))
        for d in range(1, nz):
            block = zin1.at[l, z]
            send(block, block, sent(S_Z1), z1_sem.at[l], at_z(turn(z + d, nz)))

        wait_bytes(toks2.at[l, 0, 0 : ny - 1], y2_sem.at[l])

        def ring2_send(origin, direction, half, step):
            part = toks2.at[l, origin, half * hy : (half + 1) * hy]
            send(part, part, sent(S_RING2), ring2_sem.at[l, (direction + 1) // 2, half, step - 1], at_z(turn(z + direction, nz)))

        def ring1_send(origin, direction, half, step):
            part = rows1.at[l, origin, half * hj : (half + 1) * hj]
            send(part, part, sent(S_RING1), ring1_sem.at[l, (direction + 1) // 2, half, step - 1], at_y(turn(y + direction, ny)))

        def ring2_step(step):
            for direction in (1, -1):
                origin = turn(z - direction * step, nz)
                for half in (0, 1):
                    if hops(direction, half, nz) >= step:
                        wait_bytes(
                            toks2.at[l, origin, half * hy : (half + 1) * hy],
                            ring2_sem.at[l, (direction + 1) // 2, half, step - 1],
                        )
                        if hops(direction, half, nz) > step:
                            ring2_send(origin, direction, half, step + 1)

        def ring1_step(step):
            for direction in (1, -1):
                origin = turn(y - direction * step, ny)
                for half in (0, 1):
                    if hops(direction, half, ny) >= step:
                        wait_bytes(
                            rows1.at[l, origin, half * hj : (half + 1) * hj],
                            ring1_sem.at[l, (direction + 1) // 2, half, step - 1],
                        )
                        if hops(direction, half, ny) > step:
                            ring1_send(origin, direction, half, step + 1)

        def exchange2(zc):
            chunk = flat(toks2[l, zc])
            pick = pick_matrix(chunk[:, width2 - lanes :], ny, lanes // 2)
            rows = jnp.dot(pick, chunk[:, 0:f2], preferred_element_type=F32)
            xo2[l, zc] = rows.reshape(nj, ny, f2).astype(BF16)
            rows2[l, zc, j] = xo2[l, zc, j]
            for d in range(1, nj):
                other = turn(j + d, nj)
                send(xo2.at[l, zc, other], rows2.at[l, zc, j], sent(S_X2), x2_sem.at[l, zc], at_j(other))

        def up1(yc):
            rows = flat(rows1[l, yc])
            at = pl.ds(yc * (nj * nz), nj * nz)
            result = jnp.dot(rows, up_v[l, 0:w1, :], preferred_element_type=F32)
            h1[0, at, :] = result[:, 0:lanes]
            h1[1, at, 0 : ff - lanes] = result[:, lanes:ff]
            h1[2, at, :] = lax.dot_general(rows, router_v[l, :, 0:w1], NT, preferred_element_type=F32)

        def up2(zc):
            wait_bytes(rows2.at[l, zc, 0 : nj - 1], x2_sem.at[l, zc])
            rows = flat(rows2[l, zc])
            at = pl.ds(zc * (nj * ny), nj * ny)
            result = jnp.dot(rows, up_v[l, w1 : w1 + f2, :], preferred_element_type=F32)
            h2[0, at, :] = result[:, 0:lanes]
            h2[1, at, 0 : ff - lanes] = result[:, lanes:ff]
            h2[2, at, :] = lax.dot_general(rows, router_v[l, :, w1 : w1 + f2], NT, preferred_element_type=F32)

        for direction in (1, -1):
            for half in (0, 1):
                if hops(direction, half, nz) >= 1:
                    ring2_send(z, direction, half, 1)

        wait_bytes(zin1.at[l, 0 : nz - 1], z1_sem.at[l])
        chunk1 = flat(zin1[l])
        pick = pick_matrix(chunk1[:, w1:], nz, 0)
        picked = jnp.dot(pick, chunk1[:, 0:w1], preferred_element_type=F32)
        xo1[l] = picked.reshape(nj, nz, w1).astype(BF16)
        rows1[l, y, j] = xo1[l, j]
        for d in range(1, nj):
            other = turn(j + d, nj)
            send(xo1.at[l, other], rows1.at[l, y, j], sent(S_X1), x1_sem.at[l], at_j(other))

        exchange2(z)
        wait_bytes(rows1.at[l, y, 0 : nj - 1], x1_sem.at[l])
        for direction in (1, -1):
            for half in (0, 1):
                if hops(direction, half, ny) >= 1:
                    ring1_send(y, direction, half, 1)

        @pl.when(l == 0)
        def _():
            for pair in weights:
                for copy in pair:
                    copy.wait()

        up1(y)
        steps2, steps1 = nz // 2, ny // 2
        done2 = [z]
        for step in range(1, max(steps1, steps2) + 1):
            if step <= steps2:
                ring2_step(step)
                arrived = [turn(z - step, nz)] if 2 * step == nz else [turn(z - step, nz), turn(z + step, nz)]
                for zc in arrived:
                    exchange2(zc)
                for zc in done2:
                    up2(zc)
                done2 = arrived
            if step <= steps1:
                ring1_step(step)
                for yc in [turn(y - step, ny)] if 2 * step == ny else [turn(y - step, ny), turn(y + step, ny)]:
                    up1(yc)
        for zc in done2:
            up2(zc)

        def silu(v):
            return v / (1.0 + jnp.exp(-v))

        def sigmoid(v):
            return 1.0 / (1.0 + jnp.exp(-v))

        def join1(yc, carry):
            base = pl.multiple_of(yc * (nj * nz), nj * nz)
            total = []
            for lane in range(3):
                tiles = [
                    h2[lane, pl.ds(jc * ny + yc, nz, stride=nj * ny), :] for jc in range(nj)
                ]
                total.append(h1[lane, pl.ds(base, nj * nz), :] + jnp.concatenate(tiles, axis=0))
            hid1[yc, :, 0:lanes] = silu(total[0]).astype(BF16)
            hid1[yc, :, lanes:ff] = silu(total[1])[:, 0 : ff - lanes].astype(BF16)
            gate1[yc] = sigmoid(total[2]).astype(BF16).astype(F32)
            return carry

        def join2(zc, carry):
            base = pl.multiple_of(zc * (nj * ny), nj * ny)
            total = []
            for lane in range(3):
                tiles = [
                    h1[lane, pl.ds(jc * nz + zc, ny, stride=nj * nz), :] for jc in range(nj)
                ]
                total.append(h2[lane, pl.ds(base, nj * ny), :] + jnp.concatenate(tiles, axis=0))
            hid2[zc, :, 0:lanes] = silu(total[0]).astype(BF16)
            hid2[zc, :, lanes:ff] = silu(total[1])[:, 0 : ff - lanes].astype(BF16)
            gate2[zc] = sigmoid(total[2]).astype(BF16).astype(F32)
            return carry

        lax.fori_loop(0, nz, join2, 0)
        lax.fori_loop(0, ny, join1, 0)

        def down2(zc):
            result = jnp.dot(hid2[zc], down_v[l, :, w1 : w1 + f2], preferred_element_type=F32)
            result = result * gate2[zc][:, 0:1]
            xr2o[l, zc] = result.reshape(nj, ny, f2).astype(BF16)
            xr2i[l, zc, j] = xr2o[l, zc, j]
            for d in range(1, nj):
                other = turn(j + d, nj)
                send(xr2o.at[l, zc, other], xr2i.at[l, zc, j], sent(S_XR2), xr2_sem.at[l, zc], at_j(other))

        def down1(yc):
            result = jnp.dot(hid1[yc], down_v[l, :, 0:w1], preferred_element_type=F32)
            result = result * gate1[yc][:, 0:1]
            part1[yc] = result.reshape(nj, nz, w1).astype(BF16)

        def combine2(zc):
            wait_bytes(xr2i.at[l, zc, 0 : nj - 1], xr2_sem.at[l, zc])
            place = place_matrix(flat(toks2[l, zc, :, :, width2 - lanes :]), ny, lanes // 2)
            total = jnp.dot(place, flat(xr2i[l, zc]), preferred_element_type=F32)
            comb2[zc] = total.reshape(ny, 8, f2).astype(BF16)

        def slot_of_send(moving, half, step, n):
            long, short = n // 2, n // 2 - 1
            order = []
            for m in (1, -1):
                for h in (0, 1):
                    for s in range(1, hops(-m, h, n) + 1):
                        order.append((m, h, s))
            return order.index((moving, half, step))

        def reduce_step(me, n, size, own, outgoing, incoming, sems, sent_sem, to, step):
            for moving in (1, -1):
                for half in (0, 1):
                    length = hops(-moving, half, n)
                    if length < step:
                        continue
                    dest = turn(me + moving * (length + 1 - step), n)
                    value = own[dest, half * size : (half + 1) * size]
                    slot = slot_of_send(moving, half, step, n)
                    if step > 1:
                        before = slot_of_send(moving, half, step - 1, n)
                        wait_bytes(incoming.at[l, before], sems.at[l, before])
                        value = (value.astype(F32) + incoming[l, before].astype(F32)).astype(BF16)
                    outgoing[l, slot] = value
                    send(outgoing.at[l, slot], incoming.at[l, slot], sent_sem, sems.at[l, slot], to(turn(me + moving, n)))

        def reduce_end(me, n, size, own, incoming, sems):
            halves = []
            for half in (0, 1):
                total = own[me, half * size : (half + 1) * size].astype(F32)
                for moving in (1, -1):
                    length = hops(-moving, half, n)
                    if length >= 1:
                        slot = slot_of_send(moving, half, length, n)
                        wait_bytes(incoming.at[l, slot], sems.at[l, slot])
                        total = total + incoming[l, slot].astype(F32)
                halves.append(total)
            return halves

        def by_distance(me, n):
            order = [turn(me + n // 2, n)]
            for d in range(n // 2 - 1, 0, -1):
                order += [turn(me + d, n), turn(me - d, n)]
            return order + [me]

        order2, order1 = by_distance(z, nz), by_distance(y, ny)
        first2, first1 = min(3, nz), min(3, ny)
        for zc in order2[:first2]:
            down2(zc)
        for yc in order1[:first1]:
            down1(yc)
        reduce_step(y, ny, hj, part1, rs1o, rs1i, rs1_sem, sent(S_RS1), at_y, 1)
        for zc in order2[first2:]:
            down2(zc)
        for yc in order1[first1:]:
            down1(yc)
        for zc in order2[:first2]:
            combine2(zc)
        reduce_step(z, nz, hy, comb2, rs2o, rs2i, rs2_sem, sent(S_RS2), at_z, 1)
        for step in range(2, max(steps1, steps2) + 1):
            for zc in order2[2 * step - 1 : 2 * step + 1]:
                combine2(zc)
            if step <= steps1:
                reduce_step(y, ny, hj, part1, rs1o, rs1i, rs1_sem, sent(S_RS1), at_y, step)
            if step <= steps2:
                reduce_step(z, nz, hy, comb2, rs2o, rs2i, rs2_sem, sent(S_RS2), at_z, step)

        for half, total in enumerate(reduce_end(y, ny, hj, part1, rs1i, rs1_sem)):
            xr1o[l, half * hj : (half + 1) * hj, :, 0:w1] = total.astype(BF16)
        xr1o[l, :, :, w1 : w1 + lanes] = gate1[y].reshape(nj, nz, lanes).astype(BF16)
        xr1i[l, j] = xr1o[l, j]
        for d in range(1, nj):
            other = turn(j + d, nj)
            send(xr1o.at[l, other], xr1i.at[l, j], sent(S_XR1), xr1_sem.at[l], at_j(other))

        for half, total in enumerate(reduce_end(z, nz, hy, comb2, rs2i, rs2_sem)):
            yr2o[l, half * hy : (half + 1) * hy] = total.astype(BF16)
        yr2i[l, y] = yr2o[l, y]
        for d in range(1, ny):
            other = turn(y + d, ny)
            send(yr2o.at[l, other], yr2i.at[l, y], sent(S_YR2), yr2_sem.at[l], at_y(other))

        wait_bytes(xr1i.at[l, 0 : nj - 1], xr1_sem.at[l])
        place1 = place_matrix(flat(zin1[l, :, :, w1 : w1 + lanes]), nz, 0)
        sums = jnp.dot(place1, flat(xr1i[l]), preferred_element_type=F32)
        zr1o[l, :, :, 0:w1] = sums[:, 0:w1].reshape(nz, 8, w1).astype(BF16)
        gates = sums[:, w1:]
        high = gates.astype(BF16).astype(F32)
        lane = lax.broadcasted_iota(jnp.int32, gates.shape, 1)
        pair = jnp.where(lane < lanes // 2, high, gates - high)
        zr1o[l, :, :, w1 : w1 + lanes] = pair.reshape(nz, 8, lanes).astype(BF16)
        zr1i[l, z] = zr1o[l, z]
        for d in range(1, nz):
            other = turn(z + d, nz)
            send(zr1o.at[l, other], zr1i.at[l, z], sent(S_ZR1), zr1_sem.at[l], at_z(other))

        wait_bytes(yr2i.at[l, 0 : ny - 1], yr2_sem.at[l])
        numer2 = jnp.sum(yr2i[l].astype(F32), axis=0)
        wait_bytes(zr1i.at[l, 0 : nz - 1], zr1_sem.at[l])
        both = jnp.sum(zr1i[l].astype(F32), axis=0)
        denom = both[:, w1 : w1 + 1] + both[:, w1 + lanes // 2 : w1 + lanes // 2 + 1]
        denom = jnp.maximum(denom, 0.5)
        stream[:, 0:w1] = (stream[:, 0:w1] + both[:, 0:w1] / denom).astype(BF16).astype(F32)
        stream[:, w1 : w1 + f2] = (stream[:, w1 : w1 + f2] + numer2 / denom).astype(BF16).astype(F32)

        wait_bytes(zin1.at[l, 0 : nz - 1], sent(S_Z1))
        wait_bytes(xo1.at[l, 0 : nj - 1], sent(S_X1))
        wait_bytes(rows1.at[l, 0 : ny - 1], sent(S_RING1))
        wait_bytes(toks2.at[l, 0, 0 : ny - 1], sent(S_Y2))
        wait_bytes(toks2.at[l, 0 : nz - 1], sent(S_RING2))
        wait_bytes(xo2.at[l, :, 0 : nj - 1], sent(S_X2))
        wait_bytes(rs1o.at[l], sent(S_RS1))
        wait_bytes(xr1o.at[l, 0 : nj - 1], sent(S_XR1))
        wait_bytes(zr1o.at[l, 0 : nz - 1], sent(S_ZR1))
        wait_bytes(xr2o.at[l, :, 0 : nj - 1], sent(S_XR2))
        wait_bytes(rs2o.at[l], sent(S_RS2))
        wait_bytes(yr2o.at[l, 0 : ny - 1], sent(S_YR2))
        return carry

    lax.fori_loop(0, layers, layer_body, 0)
    out[...] = stream[:, 0:features].astype(BF16)


def per_device(plane, tokens, routes, placement, up_weight, down_weight, router_weight):
    ny = lax.axis_size("dp")
    nj = plane
    nz = lax.axis_size("expert") // nj
    layers, _, features, ff = up_weight.shape
    w1 = features // 256 * 128
    f2 = features - w1
    padded = -(-features // 128) * 128
    width2 = padded - w1
    hj, hy = nj // 2, ny // 2
    dims = (ny, nz, nj, layers, features, w1, f2, ff)
    rows = ny * nz * nj
    dma = pltpu.SemaphoreType.DMA
    scratch = [
        pltpu.VMEM((8, padded), F32),
        pltpu.VMEM((layers, 2, 8, 128), F32),
        pltpu.VMEM((layers, features, ff), BF16),
        pltpu.VMEM((layers, ff, features), BF16),
        pltpu.VMEM((layers, 128, features), BF16),
        pltpu.VMEM((layers, nz, 8, w1 + 128), BF16),
        pltpu.VMEM((layers, nj, nz, w1), BF16),
        pltpu.VMEM((layers, ny, nj, nz, w1), BF16),
        pltpu.VMEM((layers, nz, ny, 8, width2), BF16),
        pltpu.VMEM((layers, nz, nj, ny, f2), BF16),
        pltpu.VMEM((layers, nz, nj, ny, f2), BF16),
        pltpu.VMEM((3, rows, 128), F32),
        pltpu.VMEM((3, rows, 128), F32),
        pltpu.VMEM((ny, nj * nz, ff), BF16),
        pltpu.VMEM((nz, nj * ny, ff), BF16),
        pltpu.VMEM((ny, nj * nz, 128), F32),
        pltpu.VMEM((nz, nj * ny, 128), F32),
        pltpu.VMEM((ny, nj, nz, w1), BF16),
        pltpu.VMEM((nz, ny, 8, f2), BF16),
        pltpu.VMEM((layers, 2 * (ny - 1), hj, nz, w1), BF16),
        pltpu.VMEM((layers, 2 * (ny - 1), hj, nz, w1), BF16),
        pltpu.VMEM((layers, nj, nz, w1 + 128), BF16),
        pltpu.VMEM((layers, nj, nz, w1 + 128), BF16),
        pltpu.VMEM((layers, nz, 8, w1 + 128), BF16),
        pltpu.VMEM((layers, nz, 8, w1 + 128), BF16),
        pltpu.VMEM((layers, nz, nj, ny, f2), BF16),
        pltpu.VMEM((layers, nz, nj, ny, f2), BF16),
        pltpu.VMEM((layers, 2 * (nz - 1), hy, 8, f2), BF16),
        pltpu.VMEM((layers, 2 * (nz - 1), hy, 8, f2), BF16),
        pltpu.VMEM((layers, ny, 8, f2), BF16),
        pltpu.VMEM((layers, ny, 8, f2), BF16),
        dma((layers, 2)),
        dma((layers, 12)),
        dma((layers,)),
        dma((layers,)),
        dma((layers, 2, 2, ny // 2)),
        dma((layers,)),
        dma((layers, 2, 2, nz // 2)),
        dma((layers, nz)),
        dma((layers, 2 * (ny - 1))),
        dma((layers,)),
        dma((layers,)),
        dma((layers, nz)),
        dma((layers, 2 * (nz - 1))),
        dma((layers,)),
    ]
    vmem = pl.BlockSpec(memory_space=pltpu.VMEM)
    hbm = pl.BlockSpec(memory_space=pl.ANY)
    return pl.pallas_call(
        functools.partial(kernel, dims),
        out_shape=jax.ShapeDtypeStruct(tokens.shape, BF16),
        in_specs=[vmem, vmem, vmem, vmem, hbm, hbm],
        out_specs=vmem,
        scratch_shapes=scratch,
        compiler_params=pltpu.CompilerParams(
            collective_id=0, has_side_effects=True, vmem_limit_bytes=66_000_000
        ),
    )(tokens, routes, placement, router_weight, up_weight, down_weight)


def solution(mesh, plane=8):
    return jax.shard_map(
        functools.partial(per_device, plane),
        mesh=mesh,
        in_specs=(
            P(("dp", "expert"), None),
            P(None, ("dp", "expert"), None),
            P(),
            P(None, "expert", None, "dp"),
            P(None, "expert", "dp", None),
            P(None, "expert", None),
        ),
        out_specs=P(("dp", "expert"), None),
        check_vma=False,
    )
```

time: 396 us -> 184 us (0.46)
  blocking collectives: 242 us -> 0 us
  Pallas kernels: 0 us -> 172 us
  waiting for transfers between devices: 71.6 us -> 0 us
  matrix products: 18.8 us -> 0 us
  starting transfers between devices: 15.4 us -> 0 us
  local copies, waits for them, and re-layouts: 26.6 us -> 12 us
  between operations: 13.4 us -> 0.01 us
  other arithmetic: 5.7 us -> 0 us
    all_to_all x4 -> x0, blocking collectives: 218 us -> none  [the longest x2 165 us: side_by_side(): lax.all_to_all(both, axis, split_axis=split_dim, concat_axis=concat_dim,...]
    pallas_call x0 -> x1, Pallas kernels: none -> 172 us  [per_device(): pl.pallas_call(functools.partial(kernel, dims), out_shape=jax.ShapeDtypeS...]
    all_gather x2 -> x0, waiting for transfers between devices: 43.5 us -> none  [layer_step(): lax.all_gather(arrived, 'dp', axis=0, tiled=True)]
    all_to_all x3 -> x0, waiting for transfers between devices: 28.1 us -> none  [the longest x2 26 us: sent_and_summed(): parts = lax.all_to_all(cut_along(value, dim, count), axis, 0, 0, tiled=True)]
    while x2 -> x0, blocking collectives: 24.1 us -> none
    dot_general x8 -> x0, matrix products: 18.8 us -> none  [the longest x2 12.5 us: layer_step(): jnp.dot(hidden, down_part[0], preferred_element_type=jnp.float32)]
    all_to_all x3 -> x0, starting transfers between devices: 15.3 us -> none  [the longest x2 7.69 us: sent_and_summed(): parts = lax.all_to_all(cut_along(value, dim, count), axis, 0, 0, tiled=True)]
    unnamed x10 -> x7, local copies, waits for them, and re-layouts: 0.63 us -> 12 us
  transfers between devices with their start and end apart: 5 -> 0, of which waited for: 5 -> 0; matrix products, arithmetic and copies ran while one was open for 3% -> 0% of each run, Pallas kernels for 0% -> 0%
where the time goes in v1:
time: 184 us
  Pallas kernels  172 us (93%)
  local copies, waits for them, and re-layouts  12 us (7%)
    pallas_call x1, Pallas kernels, per_device(): pl.pallas_call(functools.partial(kernel, dims), out_shape=jax.ShapeDtypeS...  172 us
    unnamed x7, local copies, waits for them, and re-layouts  12 us

profile of v1, /device:TPU:1, one launch (start us, length us, event | category | flops | bytes accessed | tf_op | source)
XLA Modules:
  0.0 183.6 jit_solution(5506754951962007097)
XLA Ops:
  0.0 0.0 copy-start
  0.0 1.5 copy.7.routes
  1.5 1.3 copy.8.router
  2.8 3.2 %copy.10.down = bf16[2,1,180,2880]{3,2,1,0:T(8,128)(2,1)} copy(bf16[2,1,180,2880]{3,0,2,1:T(2,128)(2,1)} %param.10) | data formatting | bytes 4147200 | tf_op args[4]
  6.0 0.0 copy-done
  6.0 4.6 %copy.9.up = bf16[2,1,2880,180]{3,2,1,0:T(8,128)(2,1)} copy(bf16[2,1,2880,180]{2,0,3,1:T(2,128)(2,1)S(1)} %copy-done) | data formatting | bytes 4147200 | tf_op args[3]
  10.6 171.6 %shard_map.64 = bf16[8,2880]{1,0:T(8,128)(2,1)} custom-call(bf16[8,2880]{1,0:T(8,128)(2,1)} %tokens.1, s32[2,8,4]{2,1,0:T(8,128)} %copy.7.routes, s32[2,64]{1,0:T(2,128)} %placement.1, bf16[2,1,2880]{2,1,0:T(2,128)(2,1)} %copy.8.router, bf16[2,1,2880,180]{3,2,1,0:T(8,128)(2,1)} %copy.9.up, bf16[2,1,180,2880]{3,2,1,0:T(8,128)(2,1)} %copy.10.down), custom_call_target="tpu_custom_call" | custom-call | tf_op jit(solution)/shard_map/pallas_call | solution.py:551
  182.2 1.4 copy.12
Async XLA Ops:
  0.0 6.0 %copy-start = (bf16[2,1,2880,180]{2,0,3,1:T(2,128)(2,1)S(1)}, bf16[2,1,2880,180]{2,0,3,1:T(2,128)(2,1)}, u32[]{:S(2)}) copy-start(bf16[2,1,2880,180]{2,0,3,1:T(2,128)(2,1)} %param.9) | copy-start | bytes 6220804

commit v2 on v1

--- a/solution.py
+++ b/solution.py
@@ -36,6 +36,8 @@
     out,
     stream,
     hot,
+    up_w,
+    down_w,
     up_v,
     down_v,
     router_v,
@@ -107,33 +109,29 @@
     for d in range(1, nj):
         pl.semaphore_signal(barrier, inc=1, device_id=at_j(turn(j + d, nj)), device_id_type=MESH)
 
-    weights = []
-    for layer in range(layers):
-        weights.append(
-            (
-                pltpu.make_async_copy(up.at[layer, 0], up_v.at[layer], weight_sem.at[layer, 0]),
-                pltpu.make_async_copy(down.at[layer, 0], down_v.at[layer], weight_sem.at[layer, 1]),
-            )
-        )
-        for copy in weights[-1]:
-            copy.start()
+    weights = [
+        pltpu.make_async_copy(up.at[0], up_w, weight_sem.at[0]),
+        pltpu.make_async_copy(down.at[0], down_w, weight_sem.at[1]),
+    ]
+    for copy in weights:
+        copy.start()
 
     for layer in range(layers):
         picks = routes[layer]
         count = placement.shape[1]
-        names = lax.broadcasted_iota(jnp.int32, (picks.shape[0], count), 1)
-        named = jnp.zeros((picks.shape[0], count), F32)
-        for k in range(picks.shape[1]):
-            named = named + jnp.where(picks[:, k : k + 1] == names, 1.0, 0.0)
+        names = lax.broadcasted_iota(jnp.int32, (count, picks.shape[1]), 0)
+        named = jnp.zeros((count, picks.shape[1]), F32)
+        for k in range(picks.shape[0]):
+            named = named + jnp.where(picks[k : k + 1, :] == names, 1.0, 0.0)
         slot_of = jnp.broadcast_to(placement[layer : layer + 1, :], (lanes, count))
         slots = lax.broadcasted_iota(jnp.int32, (lanes, count), 0)
         for which, shift in ((0, 0), (1, lanes // 2)):
             serves = jnp.where(slot_of + shift == slots, 1.0, 0.0).astype(BF16)
             hot[layer, which] = lax.dot_general(
-                named.astype(BF16), serves, NT, preferred_element_type=F32
+                named.astype(BF16), serves, (((0,), (1,)), ((), ())), preferred_element_type=F32
             )
     for layer in range(layers):
-        gate_row = jnp.broadcast_to(router[layer].astype(F32), (lanes, features)).astype(BF16)
+        gate_row = jnp.broadcast_to(router[0].astype(F32)[layer : layer + 1, :], (lanes, features)).astype(BF16)
         router_v[layer, :, 0:features] = gate_row
 
     stream[...] = jnp.zeros_like(stream)
@@ -201,6 +199,14 @@
             block = zin1.at[l, z]
             send(block, block, sent(S_Z1), z1_sem.at[l], at_z(turn(z + d, nz)))
 
+        @pl.when(l == 0)
+        def _():
+            for copy in weights:
+                copy.wait()
+            for layer in range(layers):
+                up_v[layer] = up_w[:, layer, :]
+            down_v[0] = down_w[:, 0, :]
+
         wait_bytes(toks2.at[l, 0, 0 : ny - 1], y2_sem.at[l])
 
         def ring2_send(origin, direction, half, step):
@@ -211,29 +217,42 @@
             part = rows1.at[l, origin, half * hj : (half + 1) * hj]
             send(part, part, sent(S_RING1), ring1_sem.at[l, (direction + 1) // 2, half, step - 1], at_y(turn(y + direction, ny)))
 
-        def ring2_step(step):
+        def ring_half(direction, long):
+            return 0 if (direction == 1) == long else 1
+
+        def ring2_step(step, long):
             for direction in (1, -1):
+                half = ring_half(direction, long)
                 origin = turn(z - direction * step, nz)
-                for half in (0, 1):
-                    if hops(direction, half, nz) >= step:
-                        wait_bytes(
-                            toks2.at[l, origin, half * hy : (half + 1) * hy],
-                            ring2_sem.at[l, (direction + 1) // 2, half, step - 1],
-                        )
-                        if hops(direction, half, nz) > step:
-                            ring2_send(origin, direction, half, step + 1)
-
-        def ring1_step(step):
+                if hops(direction, half, nz) >= step:
+                    wait_bytes(
+                        toks2.at[l, origin, half * hy : (half + 1) * hy],
+                        ring2_sem.at[l, (direction + 1) // 2, half, step - 1],
+                    )
+                    if hops(direction, half, nz) > step:
+                        ring2_send(origin, direction, half, step + 1)
+
+        def ring1_step(step, long):
             for direction in (1, -1):
+                half = ring_half(direction, long)
                 origin = turn(y - direction * step, ny)
-                for half in (0, 1):
-                    if hops(direction, half, ny) >= step:
-                        wait_bytes(
-                            rows1.at[l, origin, half * hj : (half + 1) * hj],
-                            ring1_sem.at[l, (direction + 1) // 2, half, step - 1],
-                        )
-                        if hops(direction, half, ny) > step:
-                            ring1_send(origin, direction, half, step + 1)
+                if hops(direction, half, ny) >= step:
+                    wait_bytes(
+                        rows1.at[l, origin, half * hj : (half + 1) * hj],
+                        ring1_sem.at[l, (direction + 1) // 2, half, step - 1],
+                    )
+                    if hops(direction, half, ny) > step:
+                        ring1_send(origin, direction, half, step + 1)
+
+        def start_ring(send_one, me, n):
+            for long in (True, False):
+                for direction in (1, -1):
+                    half = ring_half(direction, long)
+                    if hops(direction, half, n) >= 1:
+                        send_one(me, direction, half, 1)
+
+        def at_distance(me, d, n):
+            return [turn(me + d, n)] if d == 0 or 2 * d == n else [turn(me + d, n), turn(me - d, n)]
 
         def exchange2(zc):
             chunk = flat(toks2[l, zc])
@@ -248,7 +267,7 @@
         def up1(yc):
             rows = flat(rows1[l, yc])
             at = pl.ds(yc * (nj * nz), nj * nz)
-            result = jnp.dot(rows, up_v[l, 0:w1, :], preferred_element_type=F32)
+            result = lax.dot_general(rows, up_v[l, :, 0:w1], NT, preferred_element_type=F32)
             h1[0, at, :] = result[:, 0:lanes]
             h1[1, at, 0 : ff - lanes] = result[:, lanes:ff]
             h1[2, at, :] = lax.dot_general(rows, router_v[l, :, 0:w1], NT, preferred_element_type=F32)
@@ -257,15 +276,12 @@
             wait_bytes(rows2.at[l, zc, 0 : nj - 1], x2_sem.at[l, zc])
             rows = flat(rows2[l, zc])
             at = pl.ds(zc * (nj * ny), nj * ny)
-            result = jnp.dot(rows, up_v[l, w1 : w1 + f2, :], preferred_element_type=F32)
+            result = lax.dot_general(rows, up_v[l, :, w1 : w1 + f2], NT, preferred_element_type=F32)
             h2[0, at, :] = result[:, 0:lanes]
             h2[1, at, 0 : ff - lanes] = result[:, lanes:ff]
             h2[2, at, :] = lax.dot_general(rows, router_v[l, :, w1 : w1 + f2], NT, preferred_element_type=F32)
 
-        for direction in (1, -1):
-            for half in (0, 1):
-                if hops(direction, half, nz) >= 1:
-                    ring2_send(z, direction, half, 1)
+        start_ring(ring2_send, z, nz)
 
         wait_bytes(zin1.at[l, 0 : nz - 1], z1_sem.at[l])
         chunk1 = flat(zin1[l])
@@ -278,36 +294,38 @@
             send(xo1.at[l, other], rows1.at[l, y, j], sent(S_X1), x1_sem.at[l], at_j(other))
 
         exchange2(z)
-        wait_bytes(rows1.at[l, y, 0 : nj - 1], x1_sem.at[l])
-        for direction in (1, -1):
-            for half in (0, 1):
-                if hops(direction, half, ny) >= 1:
-                    ring1_send(y, direction, half, 1)
 
         @pl.when(l == 0)
         def _():
-            for pair in weights:
-                for copy in pair:
-                    copy.wait()
-
-        up1(y)
+            for layer in range(1, layers):
+                down_v[layer] = down_w[:, layer, :]
+
         steps2, steps1 = nz // 2, ny // 2
-        done2 = [z]
-        for step in range(1, max(steps1, steps2) + 1):
+        for step in range(1, max(steps2, steps1 + 1) + 1):
+            behind = step - 1
             if step <= steps2:
-                ring2_step(step)
-                arrived = [turn(z - step, nz)] if 2 * step == nz else [turn(z - step, nz), turn(z + step, nz)]
-                for zc in arrived:
+                ring2_step(step, True)
+            if step == 1:
+                wait_bytes(rows1.at[l, y, 0 : nj - 1], x1_sem.at[l])
+                start_ring(ring1_send, y, ny)
+            elif behind <= steps1:
+                ring1_step(behind, True)
+            if step <= steps2:
+                ring2_step(step, False)
+                for zc in at_distance(z, step, nz):
                     exchange2(zc)
-                for zc in done2:
+            if step == 1:
+                up1(y)
+            elif behind <= steps1:
+                ring1_step(behind, False)
+                for yc in at_distance(y, behind, ny):
+                    up1(yc)
+            if behind <= steps2:
+                for zc in at_distance(z, behind, nz):
                     up2(zc)
-                done2 = arrived
-            if step <= steps1:
-                ring1_step(step)
-                for yc in [turn(y - step, ny)] if 2 * step == ny else [turn(y - step, ny), turn(y + step, ny)]:
-                    up1(yc)
-        for zc in done2:
-            up2(zc)
+        for behind in range(max(steps2, steps1 + 1), steps2 + 1):
+            for zc in at_distance(z, behind, nz):
+                up2(zc)
 
         def silu(v):
             return v / (1.0 + jnp.exp(-v))
@@ -373,21 +391,21 @@
                         order.append((m, h, s))
             return order.index((moving, half, step))
 
-        def reduce_step(me, n, size, own, outgoing, incoming, sems, sent_sem, to, step):
+        def reduce_step(me, n, size, own, outgoing, incoming, sems, sent_sem, to, step, long):
             for moving in (1, -1):
-                for half in (0, 1):
-                    length = hops(-moving, half, n)
-                    if length < step:
-                        continue
-                    dest = turn(me + moving * (length + 1 - step), n)
-                    value = own[dest, half * size : (half + 1) * size]
-                    slot = slot_of_send(moving, half, step, n)
-                    if step > 1:
-                        before = slot_of_send(moving, half, step - 1, n)
-                        wait_bytes(incoming.at[l, before], sems.at[l, before])
-                        value = (value.astype(F32) + incoming[l, before].astype(F32)).astype(BF16)
-                    outgoing[l, slot] = value
-                    send(outgoing.at[l, slot], incoming.at[l, slot], sent_sem, sems.at[l, slot], to(turn(me + moving, n)))
+                half = ring_half(-moving, long)
+                length = hops(-moving, half, n)
+                if length < step:
+                    continue
+                dest = turn(me + moving * (length + 1 - step), n)
+                value = own[dest, half * size : (half + 1) * size]
+                slot = slot_of_send(moving, half, step, n)
+                if step > 1:
+                    before = slot_of_send(moving, half, step - 1, n)
+                    wait_bytes(incoming.at[l, before], sems.at[l, before])
+                    value = (value.astype(F32) + incoming[l, before].astype(F32)).astype(BF16)
+                outgoing[l, slot] = value
+                send(outgoing.at[l, slot], incoming.at[l, slot], sent_sem, sems.at[l, slot], to(turn(me + moving, n)))
 
         def reduce_end(me, n, size, own, incoming, sems):
             halves = []
@@ -402,48 +420,56 @@
                 halves.append(total)
             return halves
 
-        def by_distance(me, n):
-            order = [turn(me + n // 2, n)]
-            for d in range(n // 2 - 1, 0, -1):
-                order += [turn(me + d, n), turn(me - d, n)]
-            return order + [me]
-
-        order2, order1 = by_distance(z, nz), by_distance(y, ny)
-        first2, first1 = min(3, nz), min(3, ny)
-        for zc in order2[:first2]:
-            down2(zc)
-        for yc in order1[:first1]:
-            down1(yc)
-        reduce_step(y, ny, hj, part1, rs1o, rs1i, rs1_sem, sent(S_RS1), at_y, 1)
-        for zc in order2[first2:]:
-            down2(zc)
-        for yc in order1[first1:]:
-            down1(yc)
-        for zc in order2[:first2]:
-            combine2(zc)
-        reduce_step(z, nz, hy, comb2, rs2o, rs2i, rs2_sem, sent(S_RS2), at_z, 1)
-        for step in range(2, max(steps1, steps2) + 1):
-            for zc in order2[2 * step - 1 : 2 * step + 1]:
-                combine2(zc)
-            if step <= steps1:
-                reduce_step(y, ny, hj, part1, rs1o, rs1i, rs1_sem, sent(S_RS1), at_y, step)
+        def reduce1(step, long):
+            reduce_step(y, ny, hj, part1, rs1o, rs1i, rs1_sem, sent(S_RS1), at_y, step, long)
+
+        def reduce2(step, long):
+            reduce_step(z, nz, hy, comb2, rs2o, rs2i, rs2_sem, sent(S_RS2), at_z, step, long)
+
+        def finish1():
+            for half, total in enumerate(reduce_end(y, ny, hj, part1, rs1i, rs1_sem)):
+                xr1o[l, half * hj : (half + 1) * hj, :, 0:w1] = total.astype(BF16)
+            xr1o[l, :, :, w1 : w1 + lanes] = gate1[y].reshape(nj, nz, lanes).astype(BF16)
+            xr1i[l, j] = xr1o[l, j]
+            for d in range(1, nj):
+                other = turn(j + d, nj)
+                send(xr1o.at[l, other], xr1i.at[l, j], sent(S_XR1), xr1_sem.at[l], at_j(other))
+
+        combined = set()
+
+        def need2(distance):
+            for zc_at, zc in enumerate(at_distance(z, distance, nz)):
+                if (distance, zc_at) not in combined:
+                    combined.add((distance, zc_at))
+                    combine2(zc)
+
+        for d in range(steps2, steps2 - 2, -1):
+            for zc in at_distance(z, d, nz):
+                down2(zc)
+            if steps1 - steps2 + d >= 0:
+                for yc in at_distance(y, steps1 - steps2 + d, ny):
+                    down1(yc)
+            reduce1(1, d == steps2)
+        for d in range(steps2 - 2, -1, -1):
+            for zc in at_distance(z, d, nz):
+                down2(zc)
+        for d in range(steps1 - 2, -1, -1):
+            for yc in at_distance(y, d, ny):
+                down1(yc)
+        for step in range(1, max(steps1, steps2) + 1):
+            reduce1(step + 1, True)
             if step <= steps2:
-                reduce_step(z, nz, hy, comb2, rs2o, rs2i, rs2_sem, sent(S_RS2), at_z, step)
-
-        for half, total in enumerate(reduce_end(y, ny, hj, part1, rs1i, rs1_sem)):
-            xr1o[l, half * hj : (half + 1) * hj, :, 0:w1] = total.astype(BF16)
-        xr1o[l, :, :, w1 : w1 + lanes] = gate1[y].reshape(nj, nz, lanes).astype(BF16)
-        xr1i[l, j] = xr1o[l, j]
-        for d in range(1, nj):
-            other = turn(j + d, nj)
-            send(xr1o.at[l, other], xr1i.at[l, j], sent(S_XR1), xr1_sem.at[l], at_j(other))
-
-        for half, total in enumerate(reduce_end(z, nz, hy, comb2, rs2i, rs2_sem)):
-            yr2o[l, half * hy : (half + 1) * hy] = total.astype(BF16)
-        yr2i[l, y] = yr2o[l, y]
-        for d in range(1, ny):
-            other = turn(y + d, ny)
-            send(yr2o.at[l, other], yr2i.at[l, y], sent(S_YR2), yr2_sem.at[l], at_y(other))
+                need2(steps2 + 1 - step)
+                reduce2(step, True)
+            if step == steps1 - 1:
+                finish1()
+            reduce1(step + 1, False)
+            if step < steps2:
+                need2(steps2 - step)
+                reduce2(step, False)
+        if steps1 == 1:
+            finish1()
+        need2(0)
 
         wait_bytes(xr1i.at[l, 0 : nj - 1], xr1_sem.at[l])
         place1 = place_matrix(flat(zin1[l, :, :, w1 : w1 + lanes]), nz, 0)
@@ -459,6 +485,13 @@
             other = turn(z + d, nz)
             send(zr1o.at[l, other], zr1i.at[l, z], sent(S_ZR1), zr1_sem.at[l], at_z(other))
 
+        for half, total in enumerate(reduce_end(z, nz, hy, comb2, rs2i, rs2_sem)):
+            yr2o[l, half * hy : (half + 1) * hy] = total.astype(BF16)
+        yr2i[l, y] = yr2o[l, y]
+        for d in range(1, ny):
+            other = turn(y + d, ny)
+            send(yr2o.at[l, other], yr2i.at[l, y], sent(S_YR2), yr2_sem.at[l], at_y(other))
+
         wait_bytes(yr2i.at[l, 0 : ny - 1], yr2_sem.at[l])
         numer2 = jnp.sum(yr2i[l].astype(F32), axis=0)
         wait_bytes(zr1i.at[l, 0 : nz - 1], zr1_sem.at[l])
@@ -491,7 +524,7 @@
     nj = plane
     nz = lax.axis_size("expert") // nj
     layers, _, features, ff = up_weight.shape
-    w1 = features // 256 * 128
+    w1 = features // 256 * 128 + (128 if features > 1024 else 0)
     f2 = features - w1
     padded = -(-features // 128) * 128
     width2 = padded - w1
@@ -502,7 +535,9 @@
     scratch = [
         pltpu.VMEM((8, padded), F32),
         pltpu.VMEM((layers, 2, 8, 128), F32),
-        pltpu.VMEM((layers, features, ff), BF16),
+        pltpu.VMEM((ff, layers, features), BF16),
+        pltpu.VMEM((ff, layers, features), BF16),
+        pltpu.VMEM((layers, ff, features), BF16),
         pltpu.VMEM((layers, ff, features), BF16),
         pltpu.VMEM((layers, 128, features), BF16),
         pltpu.VMEM((layers, nz, 8, w1 + 128), BF16),
@@ -531,7 +566,7 @@
         pltpu.VMEM((layers, 2 * (nz - 1), hy, 8, f2), BF16),
         pltpu.VMEM((layers, ny, 8, f2), BF16),
         pltpu.VMEM((layers, ny, 8, f2), BF16),
-        dma((layers, 2)),
+        dma((2,)),
         dma((layers, 12)),
         dma((layers,)),
         dma((layers,)),
@@ -557,7 +592,14 @@
         compiler_params=pltpu.CompilerParams(
             collective_id=0, has_side_effects=True, vmem_limit_bytes=66_000_000
         ),
-    )(tokens, routes, placement, router_weight, up_weight, down_weight)
+    )(
+        tokens,
+        jnp.transpose(routes, (0, 2, 1)),
+        placement,
+        jnp.transpose(router_weight, (1, 0, 2)),
+        jnp.transpose(up_weight, (1, 3, 0, 2)),
+        jnp.transpose(down_weight, (1, 2, 0, 3)),
+    )
 
 
 def solution(mesh, plane=8):

time: 184 us -> 150 us (0.82)
  Pallas kernels: 172 us -> 148 us
  local copies, waits for them, and re-layouts: 12 us -> 1.42 us
    pallas_call x1, Pallas kernels: 172 us -> 148 us  [per_device(): pl.pallas_call(functools.partial(kernel, dims), out_shape=jax.ShapeDtypeS...]
    unnamed x7 -> x1, local copies, waits for them, and re-layouts: 12 us -> 1.42 us
where the time goes in v2:
time: 150 us
  Pallas kernels  148 us (99%)
    pallas_call x1, Pallas kernels, per_device(): pl.pallas_call(functools.partial(kernel, dims), out_shape=jax.ShapeDtypeS...  148 us

profile of v2, /device:TPU:1, one launch (start us, length us, event | category | flops | bytes accessed | tf_op | source)
XLA Modules:
  0.0 149.5 jit_solution(18271014688749876278)
XLA Ops:
  0.0 148.1 %shard_map.64 = bf16[8,2880]{1,0:T(8,128)(2,1)} custom-call(bf16[8,2880]{1,0:T(8,128)(2,1)} %tokens.1, s32[2,4,8]{2,1,0:T(4,128)} %bitcast.7, s32[2,64]{1,0:T(2,128)} %placement.1, bf16[1,2,2880]{2,1,0:T(2,128)(2,1)} %bitcast.6, bf16[1,180,2,2880]{3,2,1,0:T(2,128)(2,1)} %bitcast.4, bf16[1,180,2,2880]{3,2,1,0:T(2,128)(2,1)} %bitcast.5), custom_call_target="tpu_custom_call" | custom-call | tf_op jit(solution)/shard_map/pallas_call | solution.py:586
  148.1 1.4 copy.8

commit v3 on v2

v3 whole, which is shorter than its diff:
```python
import functools

import jax
import jax.numpy as jnp
from jax import lax
from jax.experimental import pallas as pl
from jax.experimental.pallas import tpu as pltpu
from jax.sharding import PartitionSpec as P

MESH = pl.DeviceIdType.MESH
F32, BF16 = jnp.float32, jnp.bfloat16
NT = (((1,), (1,)), ((), ()))


def flat(value):
    width = value.shape[-1]
    return value.astype(F32).reshape(-1, width).astype(BF16)


def flat32(value):
    return value.astype(F32).reshape(-1, value.shape[-1])


def hops(direction, half, n):
    return n // 2 if (direction == 1) == (half == 0) else n // 2 - 1


def kernel(
    dims,
    tokens,
    routes,
    placement,
    router,
    up,
    down,
    out,
    stream,
    hot,
    up_w,
    down_w,
    up_v,
    down_v,
    router_v,
    h1,
    h2,
    hid1,
    hid2,
    gate1,
    gate2,
    zin1,
    xo1,
    rows1,
    part1,
    rs1o,
    rs1i,
    xr1o,
    xr1i,
    zr1o,
    zr1i,
    toks2,
    xo2,
    rows2,
    comb2,
    xr2o,
    xr2i,
    rs2o,
    rs2i,
    yr2o,
    yr2i,
    weight_sem,
    send_sem,
    z1_sem,
    x1_sem,
    ring1_sem,
    y2_sem,
    ring2_sem,
    x2_sem,
    rs1_sem,
    xr1_sem,
    zr1_sem,
    xr2_sem,
    rs2_sem,
    yr2_sem,
):
    ny, nz, nj, layers, features, cuts1, cuts2, ff = dims
    hj, hy = nj // 2, ny // 2
    y = lax.axis_index("dp")
    e = lax.axis_index("expert")
    z, j = e // nj, e % nj
    lanes = 128

    def at_y(other):
        return (other, e)

    def at_z(other):
        return (y, other * nj + j)

    def at_j(other):
        return (y, z * nj + other)

    def turn(a, n):
        return lax.rem(a + 2 * n, n)

    barrier = pltpu.get_barrier_semaphore()
    for d in range(1, ny):
        pl.semaphore_signal(barrier, inc=1, device_id=at_y(turn(y + d, ny)), device_id_type=MESH)
    for d in range(1, nz):
        pl.semaphore_signal(barrier, inc=1, device_id=at_z(turn(z + d, nz)), device_id_type=MESH)
    for d in range(1, nj):
        pl.semaphore_signal(barrier, inc=1, device_id=at_j(turn(j + d, nj)), device_id_type=MESH)

    weights = [
        pltpu.make_async_copy(up.at[0], up_w, weight_sem.at[0]),
        pltpu.make_async_copy(down.at[0], down_w, weight_sem.at[1]),
    ]
    for copy in weights:
        copy.start()

    for layer in range(layers):
        picks = routes[layer]
        count = placement.shape[1]
        names = lax.broadcasted_iota(jnp.int32, (count, picks.shape[1]), 0)
        named = jnp.zeros((count, picks.shape[1]), F32)
        for k in range(picks.shape[0]):
            named = named + jnp.where(picks[k : k + 1, :] == names, 1.0, 0.0)
        slot_of = jnp.broadcast_to(placement[layer : layer + 1, :], (lanes, count))
        slots = lax.broadcasted_iota(jnp.int32, (lanes, count), 0)
        for which, shift in ((0, 0), (1, lanes // 2)):
            serves = jnp.where(slot_of + shift == slots, 1.0, 0.0).astype(BF16)
            hot[layer, which] = lax.dot_general(
                named.astype(BF16), serves, (((0,), (1,)), ((), ())), preferred_element_type=F32
            )
    for layer in range(layers):
        gate_row = jnp.broadcast_to(router[0].astype(F32)[layer : layer + 1, :], (lanes, features)).astype(BF16)
        router_v[layer, :, 0:features] = gate_row

    stream[...] = jnp.zeros_like(stream)
    stream[:, 0:features] = tokens[...].astype(F32)

    def picker(blocks, low):
        rows = nj * blocks
        tokens_in = blocks * 8
        return rows, tokens_in, low

    def pick_matrix(hots, blocks, low):
        rows, columns, low = picker(blocks, low)
        row = lax.broadcasted_iota(jnp.int32, (rows, lanes), 0)
        slot = lax.broadcasted_iota(jnp.int32, (rows, lanes), 1)
        wanted = jnp.where(slot == low + z * nj + row // blocks, 1.0, 0.0).astype(BF16)
        same = (
            lax.broadcasted_iota(jnp.int32, (rows, columns), 0) % blocks
            == lax.broadcasted_iota(jnp.int32, (rows, columns), 1) // 8
        )
        product = lax.dot_general(wanted, hots, NT, preferred_element_type=F32)
        return jnp.where(same, product, 0.0).astype(BF16)

    def place_matrix(hots, blocks, low):
        rows, columns, low = picker(blocks, low)
        row = lax.broadcasted_iota(jnp.int32, (rows, lanes), 0)
        slot = lax.broadcasted_iota(jnp.int32, (rows, lanes), 1)
        wanted = jnp.where(slot == low + z * nj + row // blocks, 1.0, 0.0).astype(BF16)
        same = (
            lax.broadcasted_iota(jnp.int32, (columns, rows), 1) % blocks
            == lax.broadcasted_iota(jnp.int32, (columns, rows), 0) // 8
        )
        product = lax.dot_general(hots, wanted, NT, preferred_element_type=F32)
        return jnp.where(same, product, 0.0).astype(BF16)

    def send(src, dst, sent, landed, device):
        pltpu.make_async_remote_copy(
            src_ref=src, dst_ref=dst, send_sem=sent, recv_sem=landed, device_id=device, device_id_type=MESH
        ).start()

    def wait_bytes(ref, sem):
        pltpu.make_async_copy(ref, ref, sem).wait()

    (S_Z1, S_X1, S_RING1, S_Y2, S_RING2, S_X2, S_RS1, S_XR1, S_ZR1, S_XR2, S_RS2, S_YR2) = range(12)

    parts = (0, 1)

    def layer_body(l, carry):
        sent = lambda which, part: send_sem.at[l, which, part]

        values = stream[...]
        mean = jnp.sum(values * values, axis=1, keepdims=True) * (1.0 / features)
        normed = values * lax.rsqrt(mean + 1e-05)
        for p in parts:
            low, high = cuts1[p]
            zin1[p][l, z, :, 0 : high - low] = normed[:, low:high].astype(BF16)
            if p == 0:
                zin1[p][l, z, :, high - low : high - low + lanes] = hot[l, 0].astype(BF16)
            low, high = cuts2[p]
            if p == 0:
                full = (high - low) // lanes * lanes
                toks2[p][l, z, y, :, 0:full] = normed[:, low : low + full].astype(BF16)
                toks2[p][l, z, y, :, full : full + lanes] = (normed[:, low + full :] + hot[l, 1]).astype(BF16)
            else:
                toks2[p][l, z, y] = normed[:, low:high].astype(BF16)

        @pl.when(l == 0)
        def _():
            pl.semaphore_wait(barrier, ny + nz + nj - 3)

        for p in parts:
            for d in range(1, ny):
                block = toks2[p].at[l, z, y]
                send(block, block, sent(S_Y2, p), y2_sem.at[l, p], at_y(turn(y + d, ny)))
            for d in range(1, nz):
                block = zin1[p].at[l, z]
                send(block, block, sent(S_Z1, p), z1_sem.at[l, p], at_z(turn(z + d, nz)))

        @pl.when(l == 0)
        def _():
            for copy in weights:
                copy.wait()
            up_v[0] = up_w[:, 0, :]
            down_v[0] = down_w[:, 0, :]

        def ring_half(direction, long):
            return 0 if (direction == 1) == long else 1

        def ring2_send(origin, direction, half, step, p):
            part = toks2[p].at[l, origin, half * hy : (half + 1) * hy]
            landed = ring2_sem.at[l, p, (direction + 1) // 2, half, step - 1]
            send(part, part, sent(S_RING2, p), landed, at_z(turn(z + direction, nz)))

        def ring1_send(origin, direction, half, step, p):
            part = rows1[p].at[l, origin, half * hj : (half + 1) * hj]
            landed = ring1_sem.at[l, p, (direction + 1) // 2, half, step - 1]
            send(part, part, sent(S_RING1, p), landed, at_y(turn(y + direction, ny)))

        def ring2_step(step, p, long):
            for direction in (1, -1):
                half = ring_half(direction, long)
                origin = turn(z - direction * step, nz)
                if hops(direction, half, nz) >= step:
                    part = toks2[p].at[l, origin, half * hy : (half + 1) * hy]
                    wait_bytes(part, ring2_sem.at[l, p, (direction + 1) // 2, half, step - 1])
                    if hops(direction, half, nz) > step:
                        ring2_send(origin, direction, half, step + 1, p)

        def ring1_step(step, p, long):
            for direction in (1, -1):
                half = ring_half(direction, long)
                origin = turn(y - direction * step, ny)
                if hops(direction, half, ny) >= step:
                    part = rows1[p].at[l, origin, half * hj : (half + 1) * hj]
                    wait_bytes(part, ring1_sem.at[l, p, (direction + 1) // 2, half, step - 1])
                    if hops(direction, half, ny) > step:
                        ring1_send(origin, direction, half, step + 1, p)

        def start_ring(send_one, me, n, p):
            for long in (True, False):
                for direction in (1, -1):
                    half = ring_half(direction, long)
                    if hops(direction, half, n) >= 1:
                        send_one(me, direction, half, 1, p)

        def at_distance(me, d, n):
            return [turn(me + d, n)] if d == 0 or 2 * d == n else [turn(me + d, n), turn(me - d, n)]

        kept = {}

        def hots2(zc):
            width = cuts2[0][1] - cuts2[0][0]
            full = width // lanes * lanes
            return flat(toks2[0][l, zc, :, :, full : full + lanes])

        def exchange2(distance, p):
            for at, zc in enumerate(at_distance(z, distance, nz)):
                if p == 0:
                    kept["pick", distance, at] = pick_matrix(hots2(zc), ny, lanes // 2)
                width = cuts2[p][1] - cuts2[p][0]
                tokens_in = flat(toks2[p][l, zc, :, :, 0:width])
                rows = jnp.dot(kept["pick", distance, at], tokens_in, preferred_element_type=F32)
                xo2[p][l, zc] = rows.reshape(nj, ny, width).astype(BF16)
                rows2[p][l, zc, j] = xo2[p][l, zc, j]
                for d in range(1, nj):
                    other = turn(j + d, nj)
                    send(xo2[p].at[l, zc, other], rows2[p].at[l, zc, j], sent(S_X2, p), x2_sem.at[l, p, zc], at_j(other))

        def products(rows, cuts):
            hidden, gate = 0.0, 0.0
            for p in parts:
                low, high = cuts[p]
                hidden += lax.dot_general(rows[p], up_v[l, :, low:high], NT, preferred_element_type=F32)
                gate += lax.dot_general(rows[p], router_v[l, :, low:high], NT, preferred_element_type=F32)
            return hidden[:, 0:lanes], hidden[:, lanes:ff], gate

        def up1(yc):
            at = pl.ds(yc * (nj * nz), nj * nz)
            first, second, gate = products([flat(rows1[p][l, yc]) for p in parts], cuts1)
            h1[0, at, :] = first
            h1[1, at, 0 : ff - lanes] = second
            h1[2, at, :] = gate

        def up2(zc):
            for p in parts:
                wait_bytes(rows2[p].at[l, zc, 0 : nj - 1], x2_sem.at[l, p, zc])
            at = pl.ds(zc * (nj * ny), nj * ny)
            first, second, gate = products([flat(rows2[p][l, zc]) for p in parts], cuts2)
            h2[0, at, :] = first
            h2[1, at, 0 : ff - lanes] = second
            h2[2, at, :] = gate

        hots1 = None
        for p in parts:
            wait_bytes(toks2[p].at[l, 0, 0 : ny - 1], y2_sem.at[l, p])
            start_ring(ring2_send, z, nz, p)
            wait_bytes(zin1[p].at[l, 0 : nz - 1], z1_sem.at[l, p])
            width = cuts1[p][1] - cuts1[p][0]
            if p == 0:
                hots1 = flat(zin1[p][l, :, :, width : width + lanes])
                pick1 = pick_matrix(hots1, nz, 0)
            picked = jnp.dot(pick1, flat(zin1[p][l, :, :, 0:width]), preferred_element_type=F32)
            xo1[p][l] = picked.reshape(nj, nz, width).astype(BF16)
            rows1[p][l, y, j] = xo1[p][l, j]
            for d in range(1, nj):
                other = turn(j + d, nj)
                send(xo1[p].at[l, other], rows1[p].at[l, y, j], sent(S_X1, p), x1_sem.at[l, p], at_j(other))
        for p in parts:
            exchange2(0, p)

        steps2, steps1 = nz // 2, ny // 2
        for step in range(1, max(steps2, steps1 + 1) + 1):
            behind = step - 1
            for p in parts:
                if step <= steps2:
                    ring2_step(step, p, True)
                if step == 1:
                    wait_bytes(rows1[p].at[l, y, 0 : nj - 1], x1_sem.at[l, p])
                    start_ring(ring1_send, y, ny, p)
                elif behind <= steps1:
                    ring1_step(behind, p, True)
                if step <= steps2:
                    ring2_step(step, p, False)
                    exchange2(step, p)
                if 1 <= behind <= steps1:
                    ring1_step(behind, p, False)
            if behind <= steps1:
                for yc in at_distance(y, behind, ny):
                    up1(yc)
            if behind <= steps2:
                for zc in at_distance(z, behind, nz):
                    up2(zc)
        for behind in range(max(steps2, steps1 + 1), steps2 + 1):
            for zc in at_distance(z, behind, nz):
                up2(zc)

        def silu(v):
            return v / (1.0 + jnp.exp(-v))

        def sigmoid(v):
            return 1.0 / (1.0 + jnp.exp(-v))

        def join(chunk, own, other, ours, theirs, hidden, gate):
            base = pl.multiple_of(chunk * (nj * theirs), nj * theirs)
            total = []
            for lane in range(3):
                tiles = [other[lane, pl.ds(jc * ours + chunk, theirs, stride=nj * ours), :] for jc in range(nj)]
                total.append(own[lane, pl.ds(base, nj * theirs), :] + jnp.concatenate(tiles, axis=0))
            hidden[chunk, :, 0:lanes] = silu(total[0]).astype(BF16)
            hidden[chunk, :, lanes:ff] = silu(total[1])[:, 0 : ff - lanes].astype(BF16)
            gate[chunk] = sigmoid(total[2]).astype(BF16).astype(F32)

        def down2(distance):
            for zc in at_distance(z, distance, nz):
                join(zc, h2, h1, nz, ny, hid2, gate2)
                for p in parts:
                    low, high = cuts2[p]
                    result = jnp.dot(hid2[zc], down_v[l, :, low:high], preferred_element_type=F32)
                    result = result * gate2[zc][:, 0:1]
                    xr2o[p][l, zc] = result.reshape(nj, ny, high - low).astype(BF16)
                    xr2i[p][l, zc, j] = xr2o[p][l, zc, j]
                    for d in range(1, nj):
                        other = turn(j + d, nj)
                        send(
                            xr2o[p].at[l, zc, other], xr2i[p].at[l, zc, j], sent(S_XR2, p), xr2_sem.at[l, p, zc], at_j(other)
                        )

        def down1(distance):
            if ("part", distance) in kept or distance < 0:
                return
            kept["part", distance] = True
            for yc in at_distance(y, distance, ny):
                join(yc, h1, h2, ny, nz, hid1, gate1)
                for p in parts:
                    low, high = cuts1[p]
                    result = jnp.dot(hid1[yc], down_v[l, :, low:high], preferred_element_type=F32)
                    result = result * gate1[yc][:, 0:1]
                    part1[p][yc] = result.reshape(nj, nz, high - low).astype(BF16)

        def need2(distance, p):
            for at, zc in enumerate(at_distance(z, distance, nz)):
                if ("sum", distance, at, p) in kept:
                    continue
                kept["sum", distance, at, p] = True
                if p == 0:
                    kept["place", distance, at] = place_matrix(hots2(zc), ny, lanes // 2)
                wait_bytes(xr2i[p].at[l, zc, 0 : nj - 1], xr2_sem.at[l, p, zc])
                total = jnp.dot(kept["place", distance, at], flat(xr2i[p][l, zc]), preferred_element_type=F32)
                comb2[p][zc] = total.reshape(ny, 8, total.shape[1]).astype(BF16)

        def slot_of_send(moving, half, step, n):
            order = []
            for m in (1, -1):
                for h in (0, 1):
                    for s in range(1, hops(-m, h, n) + 1):
                        order.append((m, h, s))
            return order.index((moving, half, step))

        def reduce_step(me, n, size, own, outgoing, incoming, sems, sent_sem, to, step, long):
            for moving in (1, -1):
                half = ring_half(-moving, long)
                length = hops(-moving, half, n)
                if length < step:
                    continue
                dest = turn(me + moving * (length + 1 - step), n)
                value = own[dest, half * size : (half + 1) * size]
                slot = slot_of_send(moving, half, step, n)
                if step > 1:
                    before = slot_of_send(moving, half, step - 1, n)
                    wait_bytes(incoming.at[l, before], sems(before))
                    value = (value.astype(F32) + incoming[l, before].astype(F32)).astype(BF16)
                outgoing[l, slot] = value
                send(outgoing.at[l, slot], incoming.at[l, slot], sent_sem, sems(slot), to(turn(me + moving, n)))

        def reduce_end(me, n, size, own, incoming, sems):
            halves = []
            for half in (0, 1):
                total = own[me, half * size : (half + 1) * size].astype(F32)
                for moving in (1, -1):
                    length = hops(-moving, half, n)
                    if length >= 1:
                        slot = slot_of_send(moving, half, length, n)
                        wait_bytes(incoming.at[l, slot], sems(slot))
                        total = total + incoming[l, slot].astype(F32)
                halves.append(total)
            return halves

        def reduce1(step, p, long):
            reduce_step(
                y, ny, hj, part1[p], rs1o[p], rs1i[p], lambda slot: rs1_sem.at[l, p, slot], sent(S_RS1, p), at_y, step, long
            )

        def reduce2(step, p, long):
            reduce_step(
                z, nz, hy, comb2[p], rs2o[p], rs2i[p], lambda slot: rs2_sem.at[l, p, slot], sent(S_RS2, p), at_z, step, long
            )

        def finish1(p):
            width = cuts1[p][1] - cuts1[p][0]
            ended = reduce_end(y, ny, hj, part1[p], rs1i[p], lambda slot: rs1_sem.at[l, p, slot])
            for half, total in enumerate(ended):
                xr1o[p][l, half * hj : (half + 1) * hj, :, 0:width] = total.astype(BF16)
            if p == 0:
                xr1o[p][l, :, :, width : width + lanes] = gate1[y].reshape(nj, nz, lanes).astype(BF16)
            xr1i[p][l, j] = xr1o[p][l, j]
            for d in range(1, nj):
                other = turn(j + d, nj)
                send(xr1o[p].at[l, other], xr1i[p].at[l, j], sent(S_XR1, p), xr1_sem.at[l, p], at_j(other))

        for d in range(steps2, steps2 - 2, -1):
            down2(d)
            down1(steps1 - steps2 + d)
            for p in parts:
                reduce1(1, p, d == steps2)
        for d in range(steps2 - 2, -1, -1):
            down2(d)
        for step in range(1, max(steps1, steps2) + 1):
            for long in (True, False):
                if step == max(steps1 - 1, 1):
                    down1(0)
                down1(steps1 - step if long else steps1 - 1 - step)
                for p in parts:
                    reduce1(step + 1, p, long)
                    distance = steps2 + 1 - step if long else steps2 - step
                    if distance >= 1:
                        need2(distance, p)
                        reduce2(step, p, long)
                if step == max(steps1 - 1, 1):
                    finish1(0 if long else 1)
        for p in parts:
            need2(0, p)

        place1 = place_matrix(flat(zin1[0][l, :, :, cuts1[0][1] : cuts1[0][1] + lanes]), nz, 0)
        for p in parts:
            width = cuts1[p][1] - cuts1[p][0]
            wait_bytes(xr1i[p].at[l, 0 : nj - 1], xr1_sem.at[l, p])
            sums = jnp.dot(place1, flat(xr1i[p][l]), preferred_element_type=F32)
            zr1o[p][l, :, :, 0:width] = sums[:, 0:width].reshape(nz, 8, width).astype(BF16)
            if p == 0:
                gates = sums[:, width:]
                rounded = gates.astype(BF16).astype(F32)
                lane = lax.broadcasted_iota(jnp.int32, gates.shape, 1)
                pair = jnp.where(lane < lanes // 2, rounded, gates - rounded)
                zr1o[p][l, :, :, width : width + lanes] = pair.reshape(nz, 8, lanes).astype(BF16)
            zr1i[p][l, z] = zr1o[p][l, z]
            for d in range(1, nz):
                other = turn(z + d, nz)
                send(zr1o[p].at[l, other], zr1i[p].at[l, z], sent(S_ZR1, p), zr1_sem.at[l, p], at_z(other))

            ended = reduce_end(z, nz, hy, comb2[p], rs2i[p], lambda slot: rs2_sem.at[l, p, slot])
            for half, total in enumerate(ended):
                yr2o[p][l, half * hy : (half + 1) * hy] = total.astype(BF16)
            yr2i[p][l, y] = yr2o[p][l, y]
            for d in range(1, ny):
                other = turn(y + d, ny)
                send(yr2o[p].at[l, other], yr2i[p].at[l, y], sent(S_YR2, p), yr2_sem.at[l, p], at_y(other))

        @pl.when(l == 0)
        def _():
            for layer in range(1, layers):
                up_v[layer] = up_w[:, layer, :]
                down_v[layer] = down_w[:, layer, :]

        denom = None
        for p in parts:
            low, high = cuts1[p]
            wait_bytes(zr1i[p].at[l, 0 : nz - 1], zr1_sem.at[l, p])
            both = jnp.sum(zr1i[p][l].astype(F32), axis=0)
            if p == 0:
                width = high - low
                denom = both[:, width : width + 1] + both[:, width + lanes // 2 : width + lanes // 2 + 1]
                denom = jnp.maximum(denom, 0.5)
            stream[:, low:high] = (stream[:, low:high] + both[:, 0 : high - low] / denom).astype(BF16).astype(F32)
            low, high = cuts2[p]
            wait_bytes(yr2i[p].at[l, 0 : ny - 1], yr2_sem.at[l, p])
            numer = jnp.sum(yr2i[p][l].astype(F32), axis=0)
            stream[:, low:high] = (stream[:, low:high] + numer / denom).astype(BF16).astype(F32)

        for p in parts:
            wait_bytes(zin1[p].at[l, 0 : nz - 1], sent(S_Z1, p))
            wait_bytes(xo1[p].at[l, 0 : nj - 1], sent(S_X1, p))
            wait_bytes(rows1[p].at[l, 0 : ny - 1], sent(S_RING1, p))
            wait_bytes(toks2[p].at[l, 0, 0 : ny - 1], sent(S_Y2, p))
            wait_bytes(toks2[p].at[l, 0 : nz - 1], sent(S_RING2, p))
            wait_bytes(xo2[p].at[l, :, 0 : nj - 1], sent(S_X2, p))
            wait_bytes(rs1o[p].at[l], sent(S_RS1, p))
            wait_bytes(xr1o[p].at[l, 0 : nj - 1], sent(S_XR1, p))
            wait_bytes(zr1o[p].at[l, 0 : nz - 1], sent(S_ZR1, p))
            wait_bytes(xr2o[p].at[l, :, 0 : nj - 1], sent(S_XR2, p))
            wait_bytes(rs2o[p].at[l], sent(S_RS2, p))
            wait_bytes(yr2o[p].at[l, 0 : ny - 1], sent(S_YR2, p))
        return carry

    lax.fori_loop(0, layers, layer_body, 0)
    out[...] = stream[:, 0:features].astype(BF16)


def per_device(plane, tokens, routes, placement, up_weight, down_weight, router_weight):
    ny = lax.axis_size("dp")
    nj = plane
    nz = lax.axis_size("expert") // nj
    layers, _, features, ff = up_weight.shape
    tiles = features // 128
    tiles1 = tiles // 2 + (1 if tiles > 8 else 0)
    first1 = tiles1 // 2 * 128
    w1 = tiles1 * 128
    second2 = w1 + (tiles - tiles1) // 2 * 128
    cuts1 = ((0, first1), (first1, w1))
    cuts2 = ((second2, features), (w1, second2))
    padded = -(-features // 128) * 128
    hj, hy = nj // 2, ny // 2
    dims = (ny, nz, nj, layers, features, cuts1, cuts2, ff)
    rows = ny * nz * nj
    dma = pltpu.SemaphoreType.DMA
    data1 = [high - low for low, high in cuts1]
    wide1 = [data1[0] + 128, data1[1]]
    data2 = [high - low for low, high in cuts2]
    wide2 = [padded - second2, data2[1]]

    def buffers(shape, widths):
        return [pltpu.VMEM((*shape, width), BF16) for width in widths]

    scratch = [
        pltpu.VMEM((8, padded), F32),
        pltpu.VMEM((layers, 2, 8, 128), F32),
        pltpu.VMEM((ff, layers, features), BF16),
        pltpu.VMEM((ff, layers, features), BF16),
        pltpu.VMEM((layers, ff, features), BF16),
        pltpu.VMEM((layers, ff, features), BF16),
        pltpu.VMEM((layers, 128, features), BF16),
        pltpu.VMEM((3, rows, 128), F32),
        pltpu.VMEM((3, rows, 128), F32),
        pltpu.VMEM((ny, nj * nz, ff), BF16),
        pltpu.VMEM((nz, nj * ny, ff), BF16),
        pltpu.VMEM((ny, nj * nz, 128), F32),
        pltpu.VMEM((nz, nj * ny, 128), F32),
        buffers((layers, nz, 8), wide1),
        buffers((layers, nj, nz), data1),
        buffers((layers, ny, nj, nz), data1),
        buffers((ny, nj, nz), data1),
        buffers((layers, 2 * (ny - 1), hj, nz), data1),
        buffers((layers, 2 * (ny - 1), hj, nz), data1),
        buffers((layers, nj, nz), wide1),
        buffers((layers, nj, nz), wide1),
        buffers((layers, nz, 8), wide1),
        buffers((layers, nz, 8), wide1),
        buffers((layers, nz, ny, 8), wide2),
        buffers((layers, nz, nj, ny), data2),
        buffers((layers, nz, nj, ny), data2),
        buffers((nz, ny, 8), data2),
        buffers((layers, nz, nj, ny), data2),
        buffers((layers, nz, nj, ny), data2),
        buffers((layers, 2 * (nz - 1), hy, 8), data2),
        buffers((layers, 2 * (nz - 1), hy, 8), data2),
        buffers((layers, ny, 8), data2),
        buffers((layers, ny, 8), data2),
        dma((2,)),
        dma((layers, 12, 2)),
        dma((layers, 2)),
        dma((layers, 2)),
        dma((layers, 2, 2, 2, ny // 2)),
        dma((layers, 2)),
        dma((layers, 2, 2, 2, nz // 2)),
        dma((layers, 2, nz)),
        dma((layers, 2, 2 * (ny - 1))),
        dma((layers, 2)),
        dma((layers, 2)),
        dma((layers, 2, nz)),
        dma((layers, 2, 2 * (nz - 1))),
        dma((layers, 2)),
    ]
    vmem = pl.BlockSpec(memory_space=pltpu.VMEM)
    hbm = pl.BlockSpec(memory_space=pl.ANY)
    return pl.pallas_call(
        functools.partial(kernel, dims),
        out_shape=jax.ShapeDtypeStruct(tokens.shape, BF16),
        in_specs=[vmem, vmem, vmem, vmem, hbm, hbm],
        out_specs=vmem,
        scratch_shapes=scratch,
        compiler_params=pltpu.CompilerParams(
            collective_id=0, has_side_effects=True, vmem_limit_bytes=66_000_000
        ),
    )(
        tokens,
        jnp.transpose(routes, (0, 2, 1)),
        placement,
        jnp.transpose(router_weight, (1, 0, 2)),
        jnp.transpose(up_weight, (1, 3, 0, 2)),
        jnp.transpose(down_weight, (1, 2, 0, 3)),
    )


def solution(mesh, plane=8):
    return jax.shard_map(
        functools.partial(per_device, plane),
        mesh=mesh,
        in_specs=(
            P(("dp", "expert"), None),
            P(None, ("dp", "expert"), None),
            P(),
            P(None, "expert", None, "dp"),
            P(None, "expert", "dp", None),
            P(None, "expert", None),
        ),
        out_specs=P(("dp", "expert"), None),
        check_vma=False,
    )
```

time: 150 us -> 143 us (0.953)
  Pallas kernels: 148 us -> 141 us
    pallas_call x1, Pallas kernels: 148 us -> 141 us  [per_device(): pl.pallas_call(functools.partial(kernel, dims), out_shape=jax.ShapeDtypeS...]
where the time goes in v3:
time: 143 us; the launch traced here: 142 us
  Pallas kernels  141 us (99%)
    pallas_call x1, Pallas kernels, per_device(): pl.pallas_call(functools.partial(kernel, dims), out_shape=jax.ShapeDtypeS...  141 us

profile of v3, /device:TPU:1, one launch (start us, length us, event | category | flops | bytes accessed | tf_op | source)
XLA Modules:
  0.0 142.5 jit_solution(1735484804313814924)
XLA Ops:
  0.0 141.1 %shard_map.64 = bf16[8,2880]{1,0:T(8,128)(2,1)} custom-call(bf16[8,2880]{1,0:T(8,128)(2,1)} %tokens.1, s32[2,4,8]{2,1,0:T(4,128)} %bitcast.7, s32[2,64]{1,0:T(2,128)} %placement.1, bf16[1,2,2880]{2,1,0:T(2,128)(2,1)} %bitcast.6, bf16[1,180,2,2880]{3,2,1,0:T(2,128)(2,1)} %bitcast.4, bf16[1,180,2,2880]{3,2,1,0:T(2,128)(2,1)} %bitcast.5), custom_call_target="tpu_custom_call" | custom-call | tf_op jit(solution)/shard_map/pallas_call | solution.py:627
  141.1 1.4 copy.8

commit v4 on v3

--- a/solution.py
+++ b/solution.py
@@ -478,8 +478,11 @@
                     if distance >= 1:
                         need2(distance, p)
                         reduce2(step, p, long)
-                if step == max(steps1 - 1, 1):
-                    finish1(0 if long else 1)
+                if step == (max(steps1 - 1, 1) if not long else steps1) and steps1 > 1:
+                    finish1(1 if long else 0)
+        if steps1 == 1:
+            finish1(0)
+            finish1(1)
         for p in parts:
             need2(0, p)
 

time: 143 us -> 143 us (level)
  no operation moved by 1% of the time
where the time goes in v4:
time: 143 us
  Pallas kernels  141 us (99%)
    pallas_call x1, Pallas kernels, per_device(): pl.pallas_call(functools.partial(kernel, dims), out_shape=jax.ShapeDtypeS...  141 us

profile of v4, /device:TPU:1, one launch (start us, length us, event | category | flops | bytes accessed | tf_op | source)
XLA Modules:
  0.0 142.5 jit_solution(15550653398032460286)
XLA Ops:
  0.0 141.1 %shard_map.64 = bf16[8,2880]{1,0:T(8,128)(2,1)} custom-call(bf16[8,2880]{1,0:T(8,128)(2,1)} %tokens.1, s32[2,4,8]{2,1,0:T(4,128)} %bitcast.7, s32[2,64]{1,0:T(2,128)} %placement.1, bf16[1,2,2880]{2,1,0:T(2,128)(2,1)} %bitcast.6, bf16[1,180,2,2880]{3,2,1,0:T(2,128)(2,1)} %bitcast.4, bf16[1,180,2,2880]{3,2,1,0:T(2,128)(2,1)} %bitcast.5), custom_call_target="tpu_custom_call" | custom-call | tf_op jit(solution)/shard_map/pallas_call | solution.py:630
  141.1 1.4 copy.8
